TPU v7x, 128 devices: a whole 4x4x4 slice. The times are simulated.
128 devices in a mesh: dp: 4 (over z), col: 4 (over y), row: 8 (over x, core).
Axes of the slice: x: 4, y: 4, z: 4, core: 2. Of those that a mesh axis runs over, the one named last changes fastest.
Arguments:
- x_attn: bfloat16 [16384, 2048], P('dp', 'row')
- dy_attn: bfloat16 [16384, 2048], P('dp', 'col')
- x_mlp: bfloat16 [16384, 2048], P('dp', 'row')
- dy_gate: bfloat16 [16384, 5120], P('dp', 'col')
- dy_up: bfloat16 [16384, 5120], P('dp', 'col')
- h_mlp: bfloat16 [16384, 5120], P('dp', 'row')
- dy_out: bfloat16 [16384, 2048], P('dp', 'col')
- w_attn: float32 [2048, 2048], P('row', 'col')
- w_gate: float32 [2048, 5120], P('row', 'col')
- w_up: float32 [2048, 5120], P('row', 'col')
- w_down: float32 [5120, 2048], P('row', 'col')
- r_attn: float32 [2048], P('row')
- c_attn: float32 [2048], P('col')
- r_gate: float32 [2048], P('row')
- c_gate: float32 [5120], P('col')
- r_up: float32 [2048], P('row')
- c_up: float32 [5120], P('col')
- r_down: float32 [5120], P('row')
- c_down: float32 [2048], P('col')
- hyper_params: float32 [3], replicated
Outputs:
- output 1: float32 [2048, 2048], P('row', 'col')
- output 2: float32 [2048], P('row')
- output 3: float32 [2048], P('col')
- output 4: float32 [2048, 5120], P('row', 'col')
- output 5: float32 [2048], P('row')
- output 6: float32 [5120], P('col')
- output 7: float32 [2048, 5120], P('row', 'col')
- output 8: float32 [2048], P('row')
- output 9: float32 [5120], P('col')
- output 10: float32 [5120, 2048], P('row', 'col')
- output 11: float32 [5120], P('row')
- output 12: float32 [2048], P('col')
All inputs are finite; a program needn't handle non-finite values.
Results may differ from a plain program's by a relative error of at most 0.001.
Values are sent between devices in bfloat16 or wider.
A program may use at most 1 GiB of HBM per device.

v0:
```python
import functools
import jax
import jax.numpy as jnp
from jax import lax
from jax.sharding import PartitionSpec as P

EPS_ONE = 1e-30
EPS_TWO = 1e-3


def matrix_step(x_block, dy_block, w_block, row_old, col_old, hyper_vals, row_size, col_size):
    beta_two = hyper_vals[0]
    rho_step = hyper_vals[1]
    clip_thr = hyper_vals[2]
    m_total = w_block.shape[0] * row_size
    n_total = w_block.shape[1] * col_size
    part_grad = jnp.einsum('tm,tn->mn', x_block, dy_block, preferred_element_type=jnp.float32)
    grad_block = lax.psum(part_grad, 'dp')
    sq_grad = grad_block * grad_block + EPS_ONE
    row_sum = lax.psum(jnp.sum(sq_grad, axis=1), 'col')
    col_sum = lax.psum(jnp.sum(sq_grad, axis=0), 'row')
    new_row = beta_two * row_old + (1.0 - beta_two) * (row_sum / n_total)
    new_col = beta_two * col_old + (1.0 - beta_two) * (col_sum / m_total)
    row_total = lax.psum(jnp.sum(new_row), 'row')
    second_est = new_row[:, None] * new_col[None, :] / row_total
    update = grad_block / jnp.sqrt(second_est)
    upd_rms = jnp.sqrt(lax.psum(jnp.sum(update * update), ('row', 'col')) / (m_total * n_total))
    update = update / jnp.maximum(1.0, upd_rms / clip_thr)
    w_rms = jnp.sqrt(lax.psum(jnp.sum(w_block * w_block), ('row', 'col')) / (m_total * n_total))
    step_size = rho_step * jnp.maximum(EPS_TWO, w_rms)
    return (w_block - step_size * update, new_row, new_col)


def solution(mesh):
    row_size = mesh.shape['row']
    col_size = mesh.shape['col']
    act_spec = P('dp', 'row')
    grad_spec = P('dp', 'col')
    w_spec = P('row', 'col')
    row_spec = P('row')
    col_spec = P('col')
    in_specs = (act_spec, grad_spec, act_spec, grad_spec, grad_spec, act_spec, grad_spec,
                w_spec, w_spec, w_spec, w_spec,
                row_spec, col_spec, row_spec, col_spec, row_spec, col_spec, row_spec, col_spec, P())
    out_specs = (w_spec, row_spec, col_spec) * 4

    def per_device(x_attn, dy_attn, x_mlp, dy_gate, dy_up, h_mlp, dy_out, w_attn, w_gate, w_up, w_down,
                   r_attn, c_attn, r_gate, c_gate, r_up, c_up, r_down, c_down, hyper_params):
        apply_one = functools.partial(matrix_step, hyper_vals=hyper_params, row_size=row_size, col_size=col_size)
        return (apply_one(x_attn, dy_attn, w_attn, r_attn, c_attn)
                + apply_one(x_mlp, dy_gate, w_gate, r_gate, c_gate)
                + apply_one(x_mlp, dy_up, w_up, r_up, c_up)
                + apply_one(h_mlp, dy_out, w_down, r_down, c_down))

    return jax.shard_map(per_device, mesh=mesh, in_specs=in_specs, out_specs=out_specs, check_vma=False)
```

profile of v0, /device:TPU:1, one launch (start us, length us, event | category | flops | bytes accessed | tf_op | source)
XLA Modules:
  0.0 267.8 jit_solution(15706793538604836010)
XLA Ops:
  7.2 0.0 copy-start
  7.2 0.0 all-reduce.6.cloned.1.call-start
  7.2 1.5 copy-done
  8.8 8.1 %fusion.14 = f32[256,1280]{1,0:T(8,128)} fusion(bf16[4096,256]{1,0:T(8,128)(2,1)S(1)} %copy-done, bf16[4096,1280]{1,0:T(8,128)(2,1)} %param.23), kind=kOutput, calls=%fused_computation.42 | convolution fusion | flops 2684354560 | bytes 13893632 | tf_op jit(solution)/shard_map/tm,tn->mn/dot_general | solution.py:17
  16.9 4.0 %fusion.15 = f32[256,1280]{1,0:T(8,128)} fusion(bf16[4096,256]{1,0:T(8,128)(2,1)S(1)} %copy-done, bf16[4096,1280]{1,0:T(8,128)(2,1)S(1)} %copy-done.1), kind=kOutput, calls=%fused_computation.43 | convolution fusion | flops 2684354560 | bytes 13893632 | tf_op jit(solution)/shard_map/tm,tn->mn/dot_general | solution.py:17
  20.9 0.0 copy-start.33
  20.9 0.0 copy-start.34
  20.9 3.9 %fusion.16 = f32[640,512]{1,0:T(8,128)} fusion(bf16[4096,640]{1,0:T(8,128)(2,1)S(1)} %bitcast.12, bf16[4096,512]{1,0:T(8,128)(2,1)S(1)} %copy-done.32), kind=kOutput, calls=%fused_computation.44 | convolution fusion | flops 2684354560 | bytes 10747904 | tf_op jit(solution)/shard_map/tm,tn->mn/dot_general | solution.py:17
  24.8 2.1 fusion.13
  26.9 0.0 all-reduce.6.cloned.1.call-update
  26.9 0.6 copy-done.25
  27.6 0.7 fusion.12
  28.9 0.0 copy-start.11
  28.9 1.9 multiply_reduce_fusion.7
  30.8 1.0 multiply_reduce_fusion.1
  31.8 0.9 multiply_reduce_fusion.3
  32.8 1.0 multiply_reduce_fusion.5
  33.7 93.5 %all-reduce.6.cloned.1.call-done = (f32[256,512]{1,0:T(8,128)}, f32[256,1280]{1,0:T(8,128)}, f32[256,1280]{1,0:T(8,128)}, f32[640,512]{1,0:T(8,128)}) async-done(((f32[256,512]{1,0:T(8,128)}, f32[256,1280]{1,0:T(8,128)}, f32[256,1280]{1,0:T(8,128)}, f32[640,512]{1,0:T(8,128)}), (f32[256,512]{1,0:T(8,128)}, f32[256,1280]{1,0:T(8,128)}, f32[256,1280]{1,0:T(8,128)}, ...) | async-done | bytes 4456464 | tf_op jit(solution)/shard_map/psum | solution.py:18
  127.2 1.8 fusion.2
  129.0 0.0 copy-start.26
  129.0 0.0 copy-start.29
  129.0 0.0 copy-start.30
  129.1 0.0 copy-start.31
  129.1 0.0 copy-start.27
  129.1 0.3 fusion
  129.4 0.3 fusion.4
  129.7 0.5 copy-done.13
  130.1 0.2 fusion.6
  130.3 8.6 %all-reduce.2 = (f32[256]{0:T(256)S(1)}, f32[256]{0:T(256)S(1)}, f32[256]{0:T(256)S(1)}, f32[640]{0:T(1024)S(1)}) all-reduce(f32[256]{0:T(256)S(1)} %get-tuple-element.19, f32[256]{0:T(256)S(1)} %get-tuple-element.17, f32[256]{0:T(256)S(1)} %get-tuple-element.15, ...), channel_id=1, replica_groups=mesh['dp'=4,'col'=4,'row'=8] {'col'}, use_global_device_ids=true, to_apply=%region_4.0 | all-reduce | flops 1408 | bytes 11264 | tf_op jit(solution)/shard_map/psum | solution.py:20
  138.9 1.2 fusion.8
  140.1 1.2 fusion.11
  141.4 1.2 fusion.9
  142.6 1.2 fusion.10
  143.9 24.1 %all-reduce.1 = (f32[]{:T(128)}, f32[512]{0:T(512)S(1)}, f32[]{:T(128)}, f32[1280]{0:T(1024)S(1)}, f32[]{:T(128)}, /*index=5*/f32[1280]{0:T(1024)S(1)}, f32[]{:T(128)}, f32[512]{0:T(512)S(1)}) all-reduce(f32[]{:T(128)} %get-tuple-element.50, f32[512]{0:T(512)S(1)} %get-tuple-element.18, ...), channel_id=1, replica_groups=mesh['dp'=4,'col'=4,'row'=8] {'row'}, use_global_device_ids=true, to_apply=%region_8.0 | all-reduce | flops 3588 | bytes 28704 | tf_op jit(solution)/shard_map/psum | solution.py:24
  168.0 0.8 multiply_add_fusion.7
  168.8 0.7 multiply_add_fusion.4
  169.4 0.0 copy-start.15
  169.5 0.7 multiply_add_fusion.5
  170.1 0.7 multiply_add_fusion.8
  170.8 2.0 multiply_reduce_fusion
  172.8 1.9 multiply_reduce_fusion.2
  174.7 1.8 multiply_reduce_fusion.4
  176.5 1.5 multiply_reduce_fusion.6
  178.0 61.9 %all-reduce = (f32[]{:T(128)}, f32[]{:T(128)}, f32[]{:T(128)}, f32[]{:T(128)}, f32[]{:T(128)}, /*index=5*/f32[]{:T(128)}, f32[]{:T(128)}, f32[]{:T(128)}) all-reduce(f32[]{:T(128)} %multiply_reduce_fusion.6, f32[]{:T(128)} %multiply_reduce_fusion.7, f32[]{:T(128)} %multiply_reduce_fusion.4, ...), channel_id=1, replica_groups=mesh['dp'=4,'col'=4,'row'=8] {'row','col'}, use_global_device_ids=true, to_apply=%region_10.0 | all-reduce | flops 8 | bytes 64 | tf_op jit(solution)/shard_map/psum | solution.py:27
  250.6 0.0 copy-start.12
  250.6 3.9 %multiply_subtract_fusion = f32[640,512]{1,0:T(8,128)} fusion(f32[640,512]{1,0:T(8,128)} %param.30, f32[]{:T(128)S(6)} %max.31, f32[]{:T(128)S(6)} %mul.261, f32[640,512]{1,0:T(8,128)S(1)} %copy-done.2, f32[]{:T(128)} %get-tuple-element.34, f32[512]{0:T(512)S(1)} %multiply_add_fusion.7, f32[640]{0:T(1024)S(1)} %get-tuple-element.45), kind=kLoop, calls=%fused_computation | loop fusion | flops 1966080 | bytes 3936780 | tf_op jit(solution)/shard_map/sub | solution.py:31
  254.5 3.0 %multiply_subtract_fusion.3 = f32[256,512]{1,0:T(8,128)} fusion(f32[256,512]{1,0:T(8,128)} %param.27, f32[]{:T(128)S(6)} %max.25, f32[]{:T(128)S(6)} %mul.213, f32[256,512]{1,0:T(8,128)} %get-tuple-element.40, f32[]{:T(128)} %get-tuple-element.28, f32[512]{0:T(512)S(1)} %multiply_add_fusion.8, f32[256]{0:T(256)S(1)} %get-tuple-element.51), kind=kLoop, calls=%fused_computation.21 | loop fusion | flops 786432 | bytes 1575948 | tf_op jit(solution)/shard_map/sub | solution.py:31
  257.5 3.4 %multiply_subtract_fusion.1 = (f32[256,1280]{1,0:T(8,128)}, f32[256,1280]{1,0:T(8,128)}) fusion(f32[256,1280]{1,0:T(8,128)S(1)} %copy-done.12, f32[]{:T(128)S(6)} %max.29, f32[]{:T(128)S(6)} %mul.248, f32[256,1280]{1,0:T(8,128)S(1)} %copy-done.7, f32[]{:T(128)} %get-tuple-element.32, f32[1280]{0:T(1024)S(1)} %multiply_add_fusion.4, ...), kind=kLoop, calls=%fused_computation.5 | loop fusion | flops 3932160 | bytes 7876632 | tf_op jit(solution)/shard_map/sub | solution.py:31
  (61 shorter events, 0.1 us)
Async XLA Ops:
  7.2 1.6 copy-start
  7.2 120.1 %all-reduce.6.cloned.1.call-start = ((), (), s32[]{:S(2)}) async-start(), calls=%async_computation | async-start | bytes 8912896 | tf_op jit(solution)/shard_map/psum | solution.py:18
  8.8 8.1 %copy-start.1 = (bf16[4096,1280]{1,0:T(8,128)(2,1)S(1)}, bf16[4096,1280]{1,0:T(8,128)(2,1)}, u32[]{:S(2)}) copy-start(bf16[4096,1280]{1,0:T(8,128)(2,1)} %param.24) | copy-start | bytes 31457284
  8.8 12.1 %slice-start = ((s8[5242880]{0:T(1024)(128)(4,1)}), s8[4194304]{0:T(1024)(128)(4,1)S(1)}, s32[]{:S(2)}) async-start(s8[5242880]{0:T(1024)(128)(4,1)} %bitcast.11), calls=%async_computation.1 | async-start | bytes 8388608
  16.9 4.0 %slice-start.1 = ((s8[5242880]{0:T(1024)(128)(4,1)}), s8[1048576]{0:T(1024)(128)(4,1)S(1)}, s32[]{:S(2)}) async-start(s8[5242880]{0:T(1024)(128)(4,1)} %bitcast.11), calls=%async_computation.2 | async-start | bytes 2097152
  16.9 4.0 %copy-start.32 = (bf16[4096,512]{1,0:T(8,128)(2,1)S(1)}, bf16[4096,512]{1,0:T(8,128)(2,1)}, u32[]{:S(2)}) copy-start(bf16[4096,512]{1,0:T(8,128)(2,1)} %param.26) | copy-start | bytes 12582916
  20.9 4.0 %copy-start.33 = (bf16[4096,512]{1,0:T(8,128)(2,1)S(1)}, bf16[4096,512]{1,0:T(8,128)(2,1)}, u32[]{:S(2)}) copy-start(bf16[4096,512]{1,0:T(8,128)(2,1)} %param.21) | copy-start | bytes 12582916
  20.9 4.0 %copy-start.34 = (bf16[4096,256]{1,0:T(8,128)(2,1)S(1)}, bf16[4096,256]{1,0:T(8,128)(2,1)}, u32[]{:S(2)}) copy-start(bf16[4096,256]{1,0:T(8,128)(2,1)} %param.20) | copy-start | bytes 6291460
  26.9 0.7 copy-start.25
  26.9 3.9 %copy-start.8 = (f32[640,512]{1,0:T(8,128)S(1)}, f32[640,512]{1,0:T(8,128)}, u32[]{:S(2)}) copy-start(f32[640,512]{1,0:T(8,128)} %param.30) | copy-start | bytes 3932164
  28.9 2.9 %copy-start.11 = (f32[256,1280]{1,0:T(8,128)S(1)}, f32[256,1280]{1,0:T(8,128)}, u32[]{:S(2)}) copy-start(f32[256,1280]{1,0:T(8,128)} %param.29) | copy-start | bytes 3932164
  30.8 2.0 copy-start.9
  127.2 1.8 copy-start.3
  127.2 2.2 copy-start.2
  129.0 1.1 copy-start.13
  129.0 9.8 %copy-start.26 = (f32[640]{0:T(1024)S(1)}, f32[640]{0:T(1024)}, u32[]{:S(2)}) copy-start(f32[640]{0:T(1024)} %param.37) | copy-start | bytes 7684
  129.0 11.1 %copy-start.29 = (f32[256]{0:T(256)S(1)}, f32[256]{0:T(256)}, u32[]{:S(2)}) copy-start(f32[256]{0:T(256)} %param.31) | copy-start | bytes 3076
  129.0 12.3 %copy-start.30 = (f32[256]{0:T(256)S(1)}, f32[256]{0:T(256)}, u32[]{:S(2)}) copy-start(f32[256]{0:T(256)} %param.35) | copy-start | bytes 3076
  129.1 13.6 %copy-start.31 = (f32[256]{0:T(256)S(1)}, f32[256]{0:T(256)}, u32[]{:S(2)}) copy-start(f32[256]{0:T(256)} %param.33) | copy-start | bytes 3076
  129.1 38.9 %copy-start.27 = (f32[512]{0:T(512)S(1)}, f32[512]{0:T(512)}, u32[]{:S(2)}) copy-start(f32[512]{0:T(512)} %param.38) | copy-start | bytes 6148
  129.1 39.7 %copy-start.23 = (f32[1280]{0:T(1024)S(1)}, f32[1280]{0:T(1024)}, u32[]{:S(2)}) copy-start(f32[1280]{0:T(1024)} %param.36) | copy-start | bytes 15364
  129.4 40.1 %copy-start.24 = (f32[1280]{0:T(1024)S(1)}, f32[1280]{0:T(1024)}, u32[]{:S(2)}) copy-start(f32[1280]{0:T(1024)} %param.34) | copy-start | bytes 15364
  129.4 40.8 %copy-start.28 = (f32[512]{0:T(512)S(1)}, f32[512]{0:T(512)}, u32[]{:S(2)}) copy-start(f32[512]{0:T(512)} %param.32) | copy-start | bytes 6148
  140.1 110.4 %copy-start.17 = (f32[640]{0:T(1024)}, f32[640]{0:T(1024)S(1)}, u32[]{:S(2)}) copy-start(f32[640]{0:T(1024)S(1)} %get-tuple-element.45) | copy-start | bytes 7684
  141.4 113.1 %copy-start.20 = (f32[256]{0:T(256)}, f32[256]{0:T(256)S(1)}, u32[]{:S(2)}) copy-start(f32[256]{0:T(256)S(1)} %get-tuple-element.51) | copy-start | bytes 3076
  142.6 114.8 %copy-start.21 = (f32[256]{0:T(256)}, f32[256]{0:T(256)S(1)}, u32[]{:S(2)}) copy-start(f32[256]{0:T(256)S(1)} %get-tuple-element.47) | copy-start | bytes 3076
  143.9 113.6 %copy-start.22 = (f32[256]{0:T(256)}, f32[256]{0:T(256)S(1)}, u32[]{:S(2)}) copy-start(f32[256]{0:T(256)S(1)} %get-tuple-element.49) | copy-start | bytes 3076
  168.0 4.8 %copy-start.6 = (f32[256,1280]{1,0:T(8,128)S(1)}, f32[256,1280]{1,0:T(8,128)}, u32[]{:S(2)}) copy-start(f32[256,1280]{1,0:T(8,128)} %get-tuple-element.42) | copy-start | bytes 3932164
  168.8 81.8 %copy-start.18 = (f32[512]{0:T(512)}, f32[512]{0:T(512)S(1)}, u32[]{:S(2)}) copy-start(f32[512]{0:T(512)S(1)} %multiply_add_fusion.7) | copy-start | bytes 6148
  169.4 88.0 %copy-start.15 = (f32[1280]{0:T(1024)}, f32[1280]{0:T(1024)S(1)}, u32[]{:S(2)}) copy-start(f32[1280]{0:T(1024)S(1)} %multiply_add_fusion.4) | copy-start | bytes 15364
  170.1 87.3 %copy-start.16 = (f32[1280]{0:T(1024)}, f32[1280]{0:T(1024)S(1)}, u32[]{:S(2)}) copy-start(f32[1280]{0:T(1024)S(1)} %multiply_add_fusion.5) | copy-start | bytes 15364
  170.8 83.7 %copy-start.19 = (f32[512]{0:T(512)}, f32[512]{0:T(512)S(1)}, u32[]{:S(2)}) copy-start(f32[512]{0:T(512)S(1)} %multiply_add_fusion.8) | copy-start | bytes 6148
  170.8 3.8 %copy-start.4 = (f32[256,1280]{1,0:T(8,128)S(1)}, f32[256,1280]{1,0:T(8,128)}, u32[]{:S(2)}) copy-start(f32[256,1280]{1,0:T(8,128)} %get-tuple-element.41) | copy-start | bytes 3932164
  172.8 3.7 %copy-start.14 = (f32[256,512]{1,0:T(8,128)S(1)}, f32[256,512]{1,0:T(8,128)}, u32[]{:S(2)}) copy-start(f32[256,512]{1,0:T(8,128)} %get-tuple-element.40) | copy-start | bytes 1572868
  250.5 6.9 %copy-start.7 = (f32[256,1280]{1,0:T(8,128)S(1)}, f32[256,1280]{1,0:T(8,128)}, u32[]{:S(2)}) copy-start(f32[256,1280]{1,0:T(8,128)} %get-tuple-element.42) | copy-start | bytes 3932164
  250.5 6.9 %copy-start.10 = (f32[256,1280]{1,0:T(8,128)S(1)}, f32[256,1280]{1,0:T(8,128)}, u32[]{:S(2)}) copy-start(f32[256,1280]{1,0:T(8,128)} %param.28) | copy-start | bytes 3932164
  250.6 6.9 %copy-start.12 = (f32[256,1280]{1,0:T(8,128)S(1)}, f32[256,1280]{1,0:T(8,128)}, u32[]{:S(2)}) copy-start(f32[256,1280]{1,0:T(8,128)} %param.29) | copy-start | bytes 3932164
  254.5 3.0 %copy-start.5 = (f32[256,1280]{1,0:T(8,128)S(1)}, f32[256,1280]{1,0:T(8,128)}, u32[]{:S(2)}) copy-start(f32[256,1280]{1,0:T(8,128)} %get-tuple-element.41) | copy-start | bytes 3932164
Sparse Core Ops, SparseCore 0:
  27.1 100.1 all-reduce.5
where the time goes:
time: 273 us; the launch traced here: 268 us
  blocking collectives  94.6 us (35%)
  waiting for transfers between devices  93.5 us (34%)
  other arithmetic  32.4 us (12%)
  between operations  25.6 us (9%)
  matrix products  18.1 us (7%)
  local copies, waits for them, and re-layouts  3.48 us (1%)
    psum x1, waiting for transfers between devices, matrix_step(): grad_block = lax.psum(part_grad, 'dp')  93.5 us
    psum x1, blocking collectives, matrix_step(): lax.psum(jnp.sum(update * update), ('row', 'col')) / (m_total * n_total)  61.9 us
    psum x1, blocking collectives, matrix_step(): row_total = lax.psum(jnp.sum(new_row), 'row')  24.1 us
    dot_general x4, matrix products, matrix_step(): jnp.einsum('tm,tn->mn', x_block, dy_block, preferred_element_type=jnp.flo...  18.1 us
    sub x3, other arithmetic, matrix_step(): return (w_block - step_size * update, new_row, new_col)  10.3 us
    psum x1, blocking collectives, matrix_step(): row_sum = lax.psum(jnp.sum(sq_grad, axis=1), 'col')  8.55 us
    reduce_sum x4, other arithmetic, matrix_step(): jnp.sum(update * update)  7.14 us
  transfers between devices with their start and end apart: 1, of which 1 were waited for; matrix products, arithmetic and copies ran while one was open for 2% of the time, Pallas kernels for 0%

commit v1 on v0

v1 whole, which is shorter than its diff:
```python
import functools
import jax
import jax.numpy as jnp
from jax import lax
from jax.experimental import pallas as pl
from jax.experimental.pallas import tpu as pltpu
from jax.sharding import PartitionSpec as P

EPS_ONE = 1e-30
EPS_TWO = 1e-3
LANES = 128
MESH = pl.DeviceIdType.MESH
N_MAT = 4
TOKEN_CHUNKS = 4


class Mat:
    def __init__(self, m, n, row_size, col_size, row_off, col_off):
        self.m, self.n = m, n
        self.mc = m // 8
        self.m_total, self.n_total = m * row_size, n * col_size
        self.rows = m // LANES
        self.row_off, self.col_off = row_off, col_off


def remote(src, dst, send_sem, recv_sem, axis, index):
    return pltpu.make_async_remote_copy(src_ref=src, dst_ref=dst, send_sem=send_sem, recv_sem=recv_sem,
                                        device_id={axis: index}, device_id_type=MESH)


def total(value):
    return jnp.sum(jnp.sum(value, axis=0, keepdims=True), axis=1, keepdims=True)


def kernel(mats, dp_size, col_size, row_size,
           x_attn, dy_attn, x_mlp, dy_gate, dy_up, h_mlp, dy_out,
           w0, w1, w2, w3, r0, r1, r2, r3, c0, c1, c2, c3, hyper,
           o0, o1, o2, o3, ro0, ro1, ro2, ro3, co0, co1, co2, co3,
           x_attn_v, dy_attn_v, x_mlp_v, dy_gate_v, dy_up_v, h_mlp_v, dy_out_v,
           wv0, wv1, wv2, wv3, gp0, gp1, gp2, gp3, gf0, gf1, gf2, gf3, rb0, rb1, rb2, rb3,
           r_old, c_old, r_new, c_new, b_row, a0, a1, a2, a3,
           cz, rz, cx, ry, sz, sy, sx,
           in_sem, w_sem, rc_sem, out_sem, rc_out_sem,
           rs_send, rs_recv, bc_send, bc_recv,
           z_send, z_recv, x_send, x_recv, y_send, y_recv):
    w_hbm = (w0, w1, w2, w3)
    r_hbm = (r0, r1, r2, r3)
    c_hbm = (c0, c1, c2, c3)
    w_out = (o0, o1, o2, o3)
    r_out = (ro0, ro1, ro2, ro3)
    c_out = (co0, co1, co2, co3)
    w_v = (wv0, wv1, wv2, wv3)
    gp = (gp0, gp1, gp2, gp3)
    gf = (gf0, gf1, gf2, gf3)
    rb = (rb0, rb1, rb2, rb3)
    acol = (a0, a1, a2, a3)
    z = lax.axis_index("dp")
    y = lax.axis_index("col")
    x = lax.axis_index("row")
    zp, zm, z2 = lax.rem(z + 1, 4), lax.rem(z + 3, 4), lax.rem(z + 2, 4)

    acts = ((x_attn, x_attn_v), (dy_attn, dy_attn_v), (x_mlp, x_mlp_v), (dy_gate, dy_gate_v),
            (dy_up, dy_up_v), (h_mlp, h_mlp_v), (dy_out, dy_out_v))
    groups = ((0, 1), (2, 3), (4,), (5, 6))
    tokens = x_attn.shape[0]
    tc = tokens // TOKEN_CHUNKS

    def act_copy(a, t):
        src, dst = acts[a]
        return pltpu.make_async_copy(src.at[pl.ds(t * tc, tc), :], dst.at[pl.ds(t * tc, tc), :], in_sem.at[a, t])

    for group in groups:
        for t in range(TOKEN_CHUNKS):
            for a in group:
                act_copy(a, t).start()
    w_copies = [pltpu.make_async_copy(w_hbm[k], w_v[k], w_sem.at[k]) for k in range(N_MAT)]
    rc_copies = []
    for k, mat in enumerate(mats):
        rc_copies.append(pltpu.make_async_copy(r_hbm[k], r_old.at[pl.ds(mat.row_off, mat.rows)], rc_sem.at[k]))
        rc_copies.append(pltpu.make_async_copy(c_hbm[k], c_old.at[:, pl.ds(mat.col_off, mat.n)], rc_sem.at[4 + k]))
    for copy in w_copies + rc_copies:
        copy.start()

    barrier = pltpu.get_barrier_semaphore()
    partners = 0
    for axis, me, size in (("dp", z, dp_size), ("col", y, col_size), ("row", x, row_size)):
        for d in range(1, size):
            pl.semaphore_signal(barrier, inc=1, device_id={axis: lax.rem(me + d, size)}, device_id_type=MESH)
            partners += 1

    operands = ((x_attn_v, dy_attn_v, (0, 1)), (x_mlp_v, dy_gate_v, (2, 3)),
                (x_mlp_v, dy_up_v, (4,)), (h_mlp_v, dy_out_v, (5, 6)))

    def matmul_chunk(k, t):
        x_ref, dy_ref, group = operands[k]
        mat = mats[k]
        for a in group:
            act_copy(a, t).wait()
        part = lax.dot_general(x_ref[pl.ds(t * tc, tc), :], dy_ref[pl.ds(t * tc, tc), :],
                               (((0,), (0,)), ((), ())), preferred_element_type=jnp.float32)
        part = part.reshape(8, mat.mc, mat.n)
        if t == 0:
            gp[k][...] = part
        else:
            gp[k][...] += part

    def cls(root, mirror):
        return 2 * root + mirror

    rs = {}

    def rs_copy(k, i, src, axis_index):
        rs[k, i] = remote(src, rb[k].at[i], rs_send.at[k, i], rs_recv.at[k, i], "dp", axis_index)
        rs[k, i].start()

    def rs_first(k):
        rs_copy(k, 0, gp[k].at[cls(z2, 0)], zm)
        rs_copy(k, 1, gp[k].at[cls(z2, 1)], zp)
        rs_copy(k, 2, gp[k].at[cls(zp, 0)], zp)
        rs_copy(k, 3, gp[k].at[cls(zm, 1)], zm)

    def rs_forward(k):
        rs[k, 0].wait_recv()
        rb[k][0] += gp[k][cls(zm, 0)]
        rs_copy(k, 4, rb[k].at[0], zm)
        rs[k, 1].wait_recv()
        rb[k][1] += gp[k][cls(zp, 1)]
        rs_copy(k, 5, rb[k].at[1], zp)

    def rs_finish(k):
        for i in (2, 4, 3, 5):
            rs[k, i].wait_recv()
        mat = mats[k]
        row_part = jnp.zeros((mat.mc, 1), jnp.float32)
        cols = jnp.zeros((1, mat.n), jnp.float32)
        row_iota = lax.broadcasted_iota(jnp.int32, (mat.mc, LANES), 0)
        lane_iota = lax.broadcasted_iota(jnp.int32, (mat.mc, LANES), 1)
        lines = [jnp.zeros((1, LANES), jnp.float32) for _ in range(mat.rows)]
        for mirror in range(2):
            own = cls(z, mirror)
            full = gp[k][own] + rb[k][2 + mirror] + rb[k][4 + mirror]
            gf[k][own] = full
            sq = full * full + EPS_ONE
            cols = cols + jnp.sum(sq, axis=0, keepdims=True)
            row_part = jnp.broadcast_to(jnp.sum(sq, axis=1, keepdims=True), (mat.mc, LANES))
            first = own * mat.mc
            for a in range(mat.rows):
                hit = (row_iota + first) == (lane_iota + a * LANES)
                lines[a] = lines[a] + jnp.sum(jnp.where(hit, row_part, 0.0), axis=0, keepdims=True)
        cz[z, :, pl.ds(mat.col_off, mat.n)] = cols
        for a in range(mat.rows):
            rz[z, mat.row_off + a] = lines[a]

    bc = {}

    def bc_copy(k, i, chunk, axis_index):
        bc[k, i] = remote(gf[k].at[chunk], gf[k].at[chunk], bc_send.at[k, i], bc_recv.at[k, i], "dp", axis_index)
        bc[k, i].start()

    def bc_first(k):
        bc_copy(k, 0, cls(z, 0), zp)
        bc_copy(k, 1, cls(z, 1), zm)
        bc_copy(k, 2, cls(z, 1), zp)
        bc_copy(k, 3, cls(z, 0), zm)

    def bc_forward(k):
        bc[k, 0].wait_recv()
        bc_copy(k, 4, cls(zm, 0), zp)
        bc[k, 1].wait_recv()
        bc_copy(k, 5, cls(zp, 1), zm)

    def exchange_start(axis, me, size, buf, send, recv, slot):
        copies = []
        for d in range(1, size):
            copies.append(remote(buf.at[me], buf.at[me], send.at[slot, d - 1], recv.at[slot, d - 1],
                                 axis, lax.rem(me + d, size)))
            copies[-1].start()
        return copies

    def recv_all(copies):
        for copy in copies:
            copy.wait_recv()

    for t in range(TOKEN_CHUNKS):
        matmul_chunk(0, t)
    pl.semaphore_wait(barrier, partners)
    rs_first(0)
    for t in range(TOKEN_CHUNKS):
        matmul_chunk(1, t)
    rs_forward(0)
    rs_first(1)
    for t in range(TOKEN_CHUNKS):
        matmul_chunk(2, t)
    rs_first(2)
    for t in range(TOKEN_CHUNKS):
        matmul_chunk(3, t)
    rs_forward(1)
    rs_first(3)
    rs_finish(0)
    for copy in w_copies + rc_copies:
        copy.wait()
    lane = lax.broadcasted_iota(jnp.int32, (1, LANES), 1)
    scal = jnp.zeros((1, LANES), jnp.float32)
    for k in range(N_MAT):
        for mirror in range(2):
            own_w = w_v[k][cls(z, mirror)]
            scal = jnp.where(lane == 4 + k, scal + total(own_w * own_w), scal)
    rs_forward(2)
    rs_finish(1)
    rs_forward(3)
    bc_first(0)
    rs_finish(2)
    rs_finish(3)
    hops = []
    zc = exchange_start("dp", z, dp_size, cz, z_send, z_recv, 0)
    zr = exchange_start("dp", z, dp_size, rz, z_send, z_recv, 1)
    bc_first(1)
    recv_all(zc)
    recv_all(zr)
    hops += zc + zr
    cx[x] = cz[0] + cz[1] + cz[2] + cz[3]
    ry[y] = rz[0] + rz[1] + rz[2] + rz[3]
    xc = exchange_start("row", x, row_size, cx, x_send, x_recv, 0)
    yr = exchange_start("col", y, col_size, ry, y_send, y_recv, 0)
    bc_forward(0)
    recv_all(xc)
    recv_all(yr)
    hops += xc + yr
    c_sum = cx[0]
    for i in range(1, row_size):
        c_sum = c_sum + cx[i]
    r_sum = ry[0]
    for i in range(1, col_size):
        r_sum = r_sum + ry[i]
    beta_two, rho_step, clip_thr = hyper[0], hyper[1], hyper[2]
    row_iota = lax.broadcasted_iota(jnp.int32, (LANES, LANES), 0)
    lane_iota = lax.broadcasted_iota(jnp.int32, (LANES, LANES), 1)
    eye = row_iota == lane_iota
    out_rc = []
    local_sum = []
    for k, mat in enumerate(mats):
        cs = slice(mat.col_off, mat.col_off + mat.n)
        new_c = beta_two * c_old[:, cs] + (1.0 - beta_two) * (c_sum[:, cs] * (1.0 / mat.m_total))
        c_new[:, cs] = new_c
        b_row[:, cs] = lax.rsqrt(new_c)
        out_rc.append(pltpu.make_async_copy(c_new.at[:, pl.ds(mat.col_off, mat.n)], c_out[k], rc_out_sem.at[4 + k]))
        lines = []
        for a in range(mat.rows):
            at = mat.row_off + a
            lines.append(beta_two * r_old[at] + (1.0 - beta_two) * (r_sum[at] * (1.0 / mat.n_total)))
            r_new[at] = lines[-1]
        out_rc.append(pltpu.make_async_copy(r_new.at[pl.ds(mat.row_off, mat.rows)], r_out[k], rc_out_sem.at[k]))
        s_loc = lines[0]
        for line in lines[1:]:
            s_loc = s_loc + line
        s_loc = jnp.sum(s_loc, axis=1, keepdims=True)
        local_sum.append(s_loc)
        for a in range(mat.rows):
            scaled = lax.rsqrt(lines[a] / s_loc)
            column = jnp.sum(jnp.where(eye, jnp.broadcast_to(scaled, (LANES, LANES)), 0.0), axis=1, keepdims=True)
            acol[k][pl.ds(a * LANES, LANES), :] = jnp.broadcast_to(column, (LANES, LANES))

    def scaled_tile(k, chunk, j):
        mat = mats[k]
        rows = pl.ds(pl.multiple_of(chunk * mat.mc, 8), mat.mc)
        cols = b_row[:, mat.col_off + j * LANES:mat.col_off + (j + 1) * LANES]
        return gf[k][chunk, :, j * LANES:(j + 1) * LANES] * acol[k][rows, :] * cols

    for k, mat in enumerate(mats):
        acc = jnp.zeros((mat.mc, LANES), jnp.float32)
        for mirror in range(2):
            for j in range(mat.n // LANES):
                upd = scaled_tile(k, cls(z, mirror), j)
                acc = acc + upd * upd
        scal = jnp.where(lane == k, total(acc), scal)
    sz[z] = scal
    zs = exchange_start("dp", z, dp_size, sz, z_send, z_recv, 2)
    bc_first(2)
    for copy in out_rc:
        copy.start()
    recv_all(zs)
    sy[y] = sz[0] + sz[1] + sz[2] + sz[3]
    ys = exchange_start("col", y, col_size, sy, y_send, y_recv, 1)
    bc_forward(1)
    bc_first(3)
    recv_all(ys)
    scal = sy[0]
    for i in range(1, col_size):
        scal = scal + sy[i]
    for k in range(N_MAT):
        scal = jnp.where(lane == 8 + k, jnp.broadcast_to(local_sum[k], (1, LANES)), scal)
    sx[x] = scal
    xs = exchange_start("row", x, row_size, sx, x_send, x_recv, 1)
    recv_all(xs)
    hops += zs + ys + xs
    table = jnp.concatenate([sx[i] for i in range(row_size)], axis=0)
    t_lane = lax.broadcasted_iota(jnp.int32, (row_size, LANES), 1)

    def pick(at):
        return jnp.sum(jnp.where(t_lane == at, table, 0.0), axis=1, keepdims=True)

    factors = []
    for k, mat in enumerate(mats):
        s_each = pick(8 + k)
        s_all = jnp.sum(s_each, axis=0, keepdims=True)
        count = 1.0 / (mat.m_total * mat.n_total)
        u_sq = jnp.sum((s_all / s_each) * pick(k), axis=0, keepdims=True)
        w_sq = jnp.sum(pick(4 + k), axis=0, keepdims=True)
        u_rms = jnp.sqrt(u_sq * count)
        w_rms = jnp.sqrt(w_sq * count)
        step = rho_step * jnp.maximum(EPS_TWO, w_rms) / jnp.maximum(1.0, u_rms / clip_thr)
        factors.append(step * jnp.sqrt(s_all / local_sum[k]))

    outs = []

    def update(k, chunk, slot):
        mat = mats[k]
        for j in range(mat.n // LANES):
            cols = slice(j * LANES, (j + 1) * LANES)
            w_v[k][chunk, :, cols] = w_v[k][chunk, :, cols] - factors[k] * scaled_tile(k, chunk, j)
        outs.append(pltpu.make_async_copy(w_v[k].at[chunk], w_out[k].at[chunk], out_sem.at[k, slot]))
        outs[-1].start()

    def update_own(k):
        update(k, cls(z, 0), 0)
        update(k, cls(z, 1), 1)

    def update_near(k):
        update(k, cls(zm, 0), 2)
        update(k, cls(zp, 1), 3)
        bc[k, 2].wait_recv()
        update(k, cls(zm, 1), 4)
        bc[k, 3].wait_recv()
        update(k, cls(zp, 0), 5)

    def update_far(k):
        bc[k, 4].wait_recv()
        update(k, cls(z2, 0), 6)
        bc[k, 5].wait_recv()
        update(k, cls(z2, 1), 7)

    bc_forward(2)
    for k in range(N_MAT):
        update_own(k)
    update_near(0)
    update_near(1)
    update_near(2)
    update_far(0)
    update_far(1)
    bc_forward(3)
    update_far(2)
    update_near(3)
    update_far(3)
    for copy in list(rs.values()) + list(bc.values()) + hops:
        copy.wait_send()
    for copy in outs + out_rc:
        copy.wait()


def fused_step(mats, dp_size, col_size, row_size, args):
    (x_attn, dy_attn, x_mlp, dy_gate, dy_up, h_mlp, dy_out, w_list, r_list, c_list, hyper) = args
    any_spec = pl.BlockSpec(memory_space=pl.ANY)
    f32 = jnp.float32
    w_in = [w.reshape(8, mat.mc, mat.n) for w, mat in zip(w_list, mats)]
    r_in = [r.reshape(mat.rows, 1, LANES) for r, mat in zip(r_list, mats)]
    c_in = [c.reshape(1, mat.n) for c, mat in zip(c_list, mats)]
    out_shape = ([jax.ShapeDtypeStruct(w.shape, f32) for w in w_in]
                 + [jax.ShapeDtypeStruct(r.shape, f32) for r in r_in]
                 + [jax.ShapeDtypeStruct(c.shape, f32) for c in c_in])
    acts = (x_attn, dy_attn, x_mlp, dy_gate, dy_up, h_mlp, dy_out)
    n_row = sum(mat.rows for mat in mats)
    n_col = sum(mat.n for mat in mats)
    scratch = ([pltpu.VMEM(a.shape, a.dtype) for a in acts]
               + [pltpu.VMEM((8, mat.mc, mat.n), f32) for mat in mats] * 3
               + [pltpu.VMEM((6, mat.mc, mat.n), f32) for mat in mats]
               + [pltpu.VMEM((n_row, 1, LANES), f32), pltpu.VMEM((1, n_col), f32)] * 2
               + [pltpu.VMEM((1, n_col), f32)]
               + [pltpu.VMEM((mat.m, LANES), f32) for mat in mats]
               + [pltpu.VMEM((dp_size, 1, n_col), f32), pltpu.VMEM((dp_size, n_row, 1, LANES), f32),
                  pltpu.VMEM((row_size, 1, n_col), f32), pltpu.VMEM((col_size, n_row, 1, LANES), f32),
                  pltpu.VMEM((dp_size, 1, LANES), f32), pltpu.VMEM((col_size, 1, LANES), f32),
                  pltpu.VMEM((row_size, 1, LANES), f32)]
               + [pltpu.SemaphoreType.DMA((7, TOKEN_CHUNKS)), pltpu.SemaphoreType.DMA((4,)),
                  pltpu.SemaphoreType.DMA((8,)), pltpu.SemaphoreType.DMA((4, 8)), pltpu.SemaphoreType.DMA((8,))]
               + [pltpu.SemaphoreType.DMA((4, 6))] * 4
               + [pltpu.SemaphoreType.DMA((3, dp_size - 1))] * 2
               + [pltpu.SemaphoreType.DMA((2, row_size - 1))] * 2
               + [pltpu.SemaphoreType.DMA((2, col_size - 1))] * 2)
    outs = pl.pallas_call(
        functools.partial(kernel, mats, dp_size, col_size, row_size),
        out_shape=out_shape,
        in_specs=[any_spec] * 19 + [pl.BlockSpec(memory_space=pltpu.SMEM)],
        out_specs=[any_spec] * 12,
        scratch_shapes=scratch,
        compiler_params=pltpu.CompilerParams(collective_id=0, has_side_effects=True, vmem_limit_bytes=67043328),
        name="adafactor_step",
    )(*acts, *w_in, *r_in, *c_in, hyper)
    new_w = [o.reshape(w.shape) for o, w in zip(outs[:4], w_list)]
    new_r = [o.reshape(r.shape) for o, r in zip(outs[4:8], r_list)]
    new_c = [o.reshape(c.shape) for o, c in zip(outs[8:], c_list)]
    return tuple(part for trio in zip(new_w, new_r, new_c) for part in trio)


def solution(mesh):
    row_size = mesh.shape['row']
    col_size = mesh.shape['col']
    dp_size = mesh.shape['dp']
    act_spec = P('dp', 'row')
    grad_spec = P('dp', 'col')
    w_spec = P('row', 'col')
    row_spec = P('row')
    col_spec = P('col')
    in_specs = (act_spec, grad_spec, act_spec, grad_spec, grad_spec, act_spec, grad_spec,
                w_spec, w_spec, w_spec, w_spec,
                row_spec, col_spec, row_spec, col_spec, row_spec, col_spec, row_spec, col_spec, P())
    out_specs = (w_spec, row_spec, col_spec) * 4

    def per_device(x_attn, dy_attn, x_mlp, dy_gate, dy_up, h_mlp, dy_out, w_attn, w_gate, w_up, w_down,
                   r_attn, c_attn, r_gate, c_gate, r_up, c_up, r_down, c_down, hyper_params):
        w_list = (w_attn, w_gate, w_up, w_down)
        mats = []
        row_off = col_off = 0
        for w in w_list:
            mats.append(Mat(w.shape[0], w.shape[1], row_size, col_size, row_off, col_off))
            row_off += mats[-1].rows
            col_off += mats[-1].n
        return fused_step(mats, dp_size, col_size, row_size,
                          (x_attn, dy_attn, x_mlp, dy_gate, dy_up, h_mlp, dy_out, w_list,
                           (r_attn, r_gate, r_up, r_down), (c_attn, c_gate, c_up, c_down), hyper_params))

    return jax.shard_map(per_device, mesh=mesh, in_specs=in_specs, out_specs=out_specs, check_vma=False)
```

time: 273 us -> 106 us (0.39); the launches traced: 268 us -> 106 us
  blocking collectives: 94.6 us -> 0 us
  waiting for transfers between devices: 93.5 us -> 0 us
  Pallas kernels: 0 us -> 86.7 us
  other arithmetic: 32.4 us -> 3.88 us
  between operations: 25.6 us -> 0.66 us
  matrix products: 18.1 us -> 0 us
  local copies, waits for them, and re-layouts: 3.48 us -> 14.8 us
    psum x3 -> x0, blocking collectives: 94.6 us -> none  [the longest x1 61.9 us: matrix_step(): lax.psum(jnp.sum(update * update), ('row', 'col')) / (m_total * n_total)]
    psum x1 -> x0, waiting for transfers between devices: 93.5 us -> none  [matrix_step(): grad_block = lax.psum(part_grad, 'dp')]
    pallas_call x0 -> x1, Pallas kernels: none -> 86.7 us  [fused_step(): pl.pallas_call(functools.partial(kernel, mats, dp_size, col_size, row_siz...]
    reduce_sum x16 -> x0, other arithmetic: 19.4 us -> none  [the longest x4 7.14 us: matrix_step(): jnp.sum(update * update)]
    dot_general x4 -> x0, matrix products: 18.1 us -> none  [matrix_step(): jnp.einsum('tm,tn->mn', x_block, dy_block, preferred_element_type=jnp.flo...]
    sub x3 -> x0, other arithmetic: 10.3 us -> none  [matrix_step(): return (w_block - step_size * update, new_row, new_col)]
    unnamed x74 -> x19, local copies, waits for them, and re-layouts: 2.82 us -> 10.9 us
    pallas_call x0 -> x3, other arithmetic: none -> 3.88 us  [fused_step(): pl.pallas_call(functools.partial(kernel, mats, dp_size, col_size, row_siz...]
  transfers between devices with their start and end apart: 1 -> 0, of which waited for: 1 -> 0; matrix products, arithmetic and copies ran while one was open for 2% -> 0% of each run, Pallas kernels for 0% -> 0%
where the time goes in v1:
time: 106 us
  Pallas kernels  86.7 us (82%)
  local copies, waits for them, and re-layouts  14.8 us (14%)
  other arithmetic  3.88 us (4%)
    pallas_call x1, Pallas kernels, fused_step(): pl.pallas_call(functools.partial(kernel, mats, dp_size, col_size, row_siz...  86.7 us
    unnamed x19, local copies, waits for them, and re-layouts  10.9 us
    pallas_call x3, other arithmetic, fused_step(): pl.pallas_call(functools.partial(kernel, mats, dp_size, col_size, row_siz...  3.88 us
    reshape x2, local copies, waits for them, and re-layouts, fused_step(): c_in = [c.reshape(1, mat.n) for c, mat in zip(c_list, mats)]  2.59 us

profile of v1, /device:TPU:1, one launch (start us, length us, event | category | flops | bytes accessed | tf_op | source)
XLA Modules:
  0.0 106.0 jit_solution(13013359915374358632)
XLA Ops:
  0.6 1.3 %reshape.105.c1 = f32[1,1280]{1,0:T(1,128)} reshape(f32[1280]{0:T(1024)} %param.34) | data formatting | bytes 10240 | tf_op jit(solution)/shard_map/reshape | solution.py:366
  1.9 1.3 %reshape.106.c2 = f32[1,1280]{1,0:T(1,128)} reshape(f32[1280]{0:T(1024)} %param.36) | data formatting | bytes 10240 | tf_op jit(solution)/shard_map/reshape | solution.py:366
  3.2 1.3 %reshape.103.r3 = f32[5,1,128]{2,1,0:T(1,128)} reshape(f32[640]{0:T(1024)} %param.37) | data formatting | bytes 5120 | tf_op jit(solution)/shard_map/reshape | solution.py:365
  4.5 86.7 %adafactor_step.1 = (f32[8,32,512]{2,1,0:T(8,128)}, f32[8,32,1280]{2,1,0:T(8,128)}, f32[8,32,1280]{2,1,0:T(8,128)}, f32[8,80,512]{2,1,0:T(8,128)}, f32[2,1,128]{...) custom-call(bf16[4096,256]{1,0:T(8,128)(2,1)} %x_attn.1, ...), custom_call_target="tpu_custom_call" | custom-call | tf_op jit(solution)/shard_map/adafactor_step/pallas_call | solution.py:389
  91.2 1.3 %reduce = f32[1280]{0:T(1024)} reduce(f32[1,1280]{1,0:T(1,128)} %get-tuple-element.29, f32[]{:T(128)} %constant), dimensions={0}, to_apply=%get-tuple-element.29.reduce_sub_computation | reduce | bytes 10244 | tf_op jit(solution)/shard_map/adafactor_step/pallas_call | solution.py:389
  92.5 1.3 %reduce.1 = f32[1280]{0:T(1024)} reduce(f32[1,1280]{1,0:T(1,128)} %get-tuple-element.32, f32[]{:T(128)} %constant), dimensions={0}, to_apply=%get-tuple-element.32.reduce_sub_computation | reduce | bytes 10244 | tf_op jit(solution)/shard_map/adafactor_step/pallas_call | solution.py:389
  93.8 1.3 %reduce.2 = f32[5,128]{1,0:T(8,128)} reduce(f32[5,1,128]{2,1,0:T(1,128)} %get-tuple-element.34, f32[]{:T(128)} %constant), dimensions={1}, to_apply=%get-tuple-element.34.reduce_sub_computation | reduce | bytes 5124 | tf_op jit(solution)/shard_map/adafactor_step/pallas_call | solution.py:389
  95.1 1.9 %copy.41 = f32[256,512]{1,0:T(8,128)} copy(f32[256,512]{1,0:T(8,128)} %bitcast.25) | data formatting | bytes 1048576
  97.0 1.2 %copy.42 = f32[256]{0:T(256)} copy(f32[256]{0:T(256)} %bitcast.37) | data formatting | bytes 2048
  98.2 1.2 %copy.43 = f32[512]{0:T(512)} copy(f32[512]{0:T(512)} %bitcast.29) | data formatting | bytes 4096
  99.4 0.0 copy-start.4
  99.4 0.0 copy-start.1
  99.4 2.6 %copy.44 = f32[256,1280]{1,0:T(8,128)} copy(f32[256,1280]{1,0:T(8,128)} %bitcast.21) | data formatting | bytes 2621440
  102.0 0.0 copy-done.4
  102.0 0.6 copy.45
  102.6 0.0 copy-done.1
  102.6 0.0 copy-start.3
  102.6 0.0 copy-start
  102.6 1.1 copy.46
  103.6 0.0 copy-done.3
  103.6 0.6 copy.47
  104.2 0.2 copy-done
  104.4 0.0 copy-start.2
  104.4 1.1 copy.48
  105.4 0.0 copy-done.2
  105.4 0.6 copy.49
Async XLA Ops:
  99.4 2.6 %copy-start.4 = (f32[2,1,128]{2,1,0:T(1,128)S(1)}, f32[2,1,128]{2,1,0:T(1,128)}, u32[]{:S(2)}) copy-start(f32[2,1,128]{2,1,0:T(1,128)} %get-tuple-element.28) | copy-start | bytes 3076
  99.4 3.1 %copy-start.1 = (f32[8,32,1280]{2,1,0:T(8,128)S(1)}, f32[8,32,1280]{2,1,0:T(8,128)}, u32[]{:S(2)}) copy-start(f32[8,32,1280]{2,1,0:T(8,128)} %get-tuple-element.30) | copy-start | bytes 3932164
  102.6 1.1 %copy-start.3 = (f32[2,1,128]{2,1,0:T(1,128)S(1)}, f32[2,1,128]{2,1,0:T(1,128)}, u32[]{:S(2)}) copy-start(f32[2,1,128]{2,1,0:T(1,128)} %get-tuple-element.31) | copy-start | bytes 3076
  102.6 1.8 %copy-start = (f32[8,80,512]{2,1,0:T(8,128)S(1)}, f32[8,80,512]{2,1,0:T(8,128)}, u32[]{:S(2)}) copy-start(f32[8,80,512]{2,1,0:T(8,128)} %get-tuple-element.33) | copy-start | bytes 3932164
  104.4 1.1 %copy-start.2 = (f32[1,512]{1,0:T(1,128)S(1)}, f32[1,512]{1,0:T(1,128)}, u32[]{:S(2)}) copy-start(f32[1,512]{1,0:T(1,128)} %get-tuple-element.35) | copy-start | bytes 6148

commit v2 on v1

--- a/solution.py
+++ b/solution.py
@@ -12,6 +12,8 @@
 MESH = pl.DeviceIdType.MESH
 N_MAT = 4
 TOKEN_CHUNKS = 4
+VMEM_LIMIT = 58 * 1024 * 1024
+WRITE_LIMIT = 16 * 1024 * 1024
 
 
 class Mat:
@@ -35,20 +37,17 @@
 def kernel(mats, dp_size, col_size, row_size,
            x_attn, dy_attn, x_mlp, dy_gate, dy_up, h_mlp, dy_out,
            w0, w1, w2, w3, r0, r1, r2, r3, c0, c1, c2, c3, hyper,
-           o0, o1, o2, o3, ro0, ro1, ro2, ro3, co0, co1, co2, co3,
+           wv0, wv1, wv2, wv3, r_new, c_new,
            x_attn_v, dy_attn_v, x_mlp_v, dy_gate_v, dy_up_v, h_mlp_v, dy_out_v,
-           wv0, wv1, wv2, wv3, gp0, gp1, gp2, gp3, gf0, gf1, gf2, gf3, rb0, rb1, rb2, rb3,
-           r_old, c_old, r_new, c_new, b_row, a0, a1, a2, a3,
+           gp0, gp1, gp2, gp3, gf0, gf1, gf2, gf3, rb0, rb1, rb2, rb3,
+           r_old, c_old, b_row, a0, a1, a2, a3,
            cz, rz, cx, ry, sz, sy, sx,
-           in_sem, w_sem, rc_sem, out_sem, rc_out_sem,
+           in_sem, w_sem, r_sem, c_sem,
            rs_send, rs_recv, bc_send, bc_recv,
            z_send, z_recv, x_send, x_recv, y_send, y_recv):
     w_hbm = (w0, w1, w2, w3)
     r_hbm = (r0, r1, r2, r3)
     c_hbm = (c0, c1, c2, c3)
-    w_out = (o0, o1, o2, o3)
-    r_out = (ro0, ro1, ro2, ro3)
-    c_out = (co0, co1, co2, co3)
     w_v = (wv0, wv1, wv2, wv3)
     gp = (gp0, gp1, gp2, gp3)
     gf = (gf0, gf1, gf2, gf3)
@@ -76,8 +75,10 @@
     w_copies = [pltpu.make_async_copy(w_hbm[k], w_v[k], w_sem.at[k]) for k in range(N_MAT)]
     rc_copies = []
     for k, mat in enumerate(mats):
-        rc_copies.append(pltpu.make_async_copy(r_hbm[k], r_old.at[pl.ds(mat.row_off, mat.rows)], rc_sem.at[k]))
-        rc_copies.append(pltpu.make_async_copy(c_hbm[k], c_old.at[:, pl.ds(mat.col_off, mat.n)], rc_sem.at[4 + k]))
+        for a in range(mat.rows):
+            at = mat.row_off + a
+            rc_copies.append(pltpu.make_async_copy(r_hbm[k].at[pl.ds(a * LANES, LANES)], r_old.at[at, 0], r_sem.at[at]))
+        rc_copies.append(pltpu.make_async_copy(c_hbm[k], c_old.at[0, pl.ds(mat.col_off, mat.n)], c_sem.at[k]))
     for copy in w_copies + rc_copies:
         copy.start()
 
@@ -236,20 +237,17 @@
     row_iota = lax.broadcasted_iota(jnp.int32, (LANES, LANES), 0)
     lane_iota = lax.broadcasted_iota(jnp.int32, (LANES, LANES), 1)
     eye = row_iota == lane_iota
-    out_rc = []
     local_sum = []
     for k, mat in enumerate(mats):
         cs = slice(mat.col_off, mat.col_off + mat.n)
         new_c = beta_two * c_old[:, cs] + (1.0 - beta_two) * (c_sum[:, cs] * (1.0 / mat.m_total))
         c_new[:, cs] = new_c
         b_row[:, cs] = lax.rsqrt(new_c)
-        out_rc.append(pltpu.make_async_copy(c_new.at[:, pl.ds(mat.col_off, mat.n)], c_out[k], rc_out_sem.at[4 + k]))
         lines = []
         for a in range(mat.rows):
             at = mat.row_off + a
             lines.append(beta_two * r_old[at] + (1.0 - beta_two) * (r_sum[at] * (1.0 / mat.n_total)))
             r_new[at] = lines[-1]
-        out_rc.append(pltpu.make_async_copy(r_new.at[pl.ds(mat.row_off, mat.rows)], r_out[k], rc_out_sem.at[k]))
         s_loc = lines[0]
         for line in lines[1:]:
             s_loc = s_loc + line
@@ -276,8 +274,6 @@
     sz[z] = scal
     zs = exchange_start("dp", z, dp_size, sz, z_send, z_recv, 2)
     bc_first(2)
-    for copy in out_rc:
-        copy.start()
     recv_all(zs)
     sy[y] = sz[0] + sz[1] + sz[2] + sz[3]
     ys = exchange_start("col", y, col_size, sy, y_send, y_recv, 1)
@@ -311,33 +307,29 @@
         step = rho_step * jnp.maximum(EPS_TWO, w_rms) / jnp.maximum(1.0, u_rms / clip_thr)
         factors.append(step * jnp.sqrt(s_all / local_sum[k]))
 
-    outs = []
-
-    def update(k, chunk, slot):
+    def update(k, chunk):
         mat = mats[k]
         for j in range(mat.n // LANES):
             cols = slice(j * LANES, (j + 1) * LANES)
             w_v[k][chunk, :, cols] = w_v[k][chunk, :, cols] - factors[k] * scaled_tile(k, chunk, j)
-        outs.append(pltpu.make_async_copy(w_v[k].at[chunk], w_out[k].at[chunk], out_sem.at[k, slot]))
-        outs[-1].start()
 
     def update_own(k):
-        update(k, cls(z, 0), 0)
-        update(k, cls(z, 1), 1)
+        update(k, cls(z, 0))
+        update(k, cls(z, 1))
 
     def update_near(k):
-        update(k, cls(zm, 0), 2)
-        update(k, cls(zp, 1), 3)
+        update(k, cls(zm, 0))
+        update(k, cls(zp, 1))
         bc[k, 2].wait_recv()
-        update(k, cls(zm, 1), 4)
+        update(k, cls(zm, 1))
         bc[k, 3].wait_recv()
-        update(k, cls(zp, 0), 5)
+        update(k, cls(zp, 0))
 
     def update_far(k):
         bc[k, 4].wait_recv()
-        update(k, cls(z2, 0), 6)
+        update(k, cls(z2, 0))
         bc[k, 5].wait_recv()
-        update(k, cls(z2, 1), 7)
+        update(k, cls(z2, 1))
 
     bc_forward(2)
     for k in range(N_MAT):
@@ -353,52 +345,73 @@
     update_far(3)
     for copy in list(rs.values()) + list(bc.values()) + hops:
         copy.wait_send()
-    for copy in outs + out_rc:
+
+
+def write_kernel(mats, w0, w1, w2, w3, r_new, c_new,
+                 o0, o1, o2, o3, ro0, ro1, ro2, ro3, co0, co1, co2, co3, w_sem, r_sem, c_sem):
+    copies = [pltpu.make_async_copy(src, dst, w_sem.at[k])
+              for k, (src, dst) in enumerate(zip((w0, w1, w2, w3), (o0, o1, o2, o3)))]
+    for k, mat in enumerate(mats):
+        r_out = (ro0, ro1, ro2, ro3)[k]
+        c_out = (co0, co1, co2, co3)[k]
+        for a in range(mat.rows):
+            at = mat.row_off + a
+            copies.append(pltpu.make_async_copy(r_new.at[at, 0], r_out.at[pl.ds(a * LANES, LANES)], r_sem.at[at]))
+        copies.append(pltpu.make_async_copy(c_new.at[0, pl.ds(mat.col_off, mat.n)], c_out, c_sem.at[k]))
+    for copy in copies:
+        copy.start()
+    for copy in copies:
         copy.wait()
 
 
 def fused_step(mats, dp_size, col_size, row_size, args):
     (x_attn, dy_attn, x_mlp, dy_gate, dy_up, h_mlp, dy_out, w_list, r_list, c_list, hyper) = args
     any_spec = pl.BlockSpec(memory_space=pl.ANY)
+    vmem_spec = pl.BlockSpec(memory_space=pltpu.VMEM)
     f32 = jnp.float32
     w_in = [w.reshape(8, mat.mc, mat.n) for w, mat in zip(w_list, mats)]
-    r_in = [r.reshape(mat.rows, 1, LANES) for r, mat in zip(r_list, mats)]
-    c_in = [c.reshape(1, mat.n) for c, mat in zip(c_list, mats)]
-    out_shape = ([jax.ShapeDtypeStruct(w.shape, f32) for w in w_in]
-                 + [jax.ShapeDtypeStruct(r.shape, f32) for r in r_in]
-                 + [jax.ShapeDtypeStruct(c.shape, f32) for c in c_in])
     acts = (x_attn, dy_attn, x_mlp, dy_gate, dy_up, h_mlp, dy_out)
     n_row = sum(mat.rows for mat in mats)
     n_col = sum(mat.n for mat in mats)
+    w_shape = [jax.ShapeDtypeStruct(w.shape, f32) for w in w_in]
+    w_held = [pltpu.VMEM(w.shape, f32) for w in w_in]
+    packed_shape = [pltpu.VMEM((n_row, 1, LANES), f32), pltpu.VMEM((1, n_col), f32)]
     scratch = ([pltpu.VMEM(a.shape, a.dtype) for a in acts]
-               + [pltpu.VMEM((8, mat.mc, mat.n), f32) for mat in mats] * 3
+               + [pltpu.VMEM((8, mat.mc, mat.n), f32) for mat in mats] * 2
                + [pltpu.VMEM((6, mat.mc, mat.n), f32) for mat in mats]
-               + [pltpu.VMEM((n_row, 1, LANES), f32), pltpu.VMEM((1, n_col), f32)] * 2
-               + [pltpu.VMEM((1, n_col), f32)]
+               + [pltpu.VMEM((n_row, 1, LANES), f32), pltpu.VMEM((1, n_col), f32), pltpu.VMEM((1, n_col), f32)]
                + [pltpu.VMEM((mat.m, LANES), f32) for mat in mats]
                + [pltpu.VMEM((dp_size, 1, n_col), f32), pltpu.VMEM((dp_size, n_row, 1, LANES), f32),
                   pltpu.VMEM((row_size, 1, n_col), f32), pltpu.VMEM((col_size, n_row, 1, LANES), f32),
                   pltpu.VMEM((dp_size, 1, LANES), f32), pltpu.VMEM((col_size, 1, LANES), f32),
                   pltpu.VMEM((row_size, 1, LANES), f32)]
                + [pltpu.SemaphoreType.DMA((7, TOKEN_CHUNKS)), pltpu.SemaphoreType.DMA((4,)),
-                  pltpu.SemaphoreType.DMA((8,)), pltpu.SemaphoreType.DMA((4, 8)), pltpu.SemaphoreType.DMA((8,))]
+                  pltpu.SemaphoreType.DMA((n_row,)), pltpu.SemaphoreType.DMA((4,))]
                + [pltpu.SemaphoreType.DMA((4, 6))] * 4
                + [pltpu.SemaphoreType.DMA((3, dp_size - 1))] * 2
                + [pltpu.SemaphoreType.DMA((2, row_size - 1))] * 2
                + [pltpu.SemaphoreType.DMA((2, col_size - 1))] * 2)
+    held = pl.pallas_call(
+        functools.partial(kernel, mats, dp_size, col_size, row_size),
+        out_shape=w_held + packed_shape,
+        in_specs=[any_spec] * 19 + [pl.BlockSpec(memory_space=pltpu.SMEM)],
+        out_specs=[vmem_spec] * 6,
+        scratch_shapes=scratch,
+        compiler_params=pltpu.CompilerParams(collective_id=0, has_side_effects=True, vmem_limit_bytes=VMEM_LIMIT),
+        name="adafactor_step",
+    )(*acts, *w_in, *r_list, *c_list, hyper)
     outs = pl.pallas_call(
-        functools.partial(kernel, mats, dp_size, col_size, row_size),
-        out_shape=out_shape,
-        in_specs=[any_spec] * 19 + [pl.BlockSpec(memory_space=pltpu.SMEM)],
+        functools.partial(write_kernel, mats),
+        out_shape=(w_shape + [jax.ShapeDtypeStruct(r.shape, f32) for r in r_list]
+                   + [jax.ShapeDtypeStruct(c.shape, f32) for c in c_list]),
+        in_specs=[vmem_spec] * 6,
         out_specs=[any_spec] * 12,
-        scratch_shapes=scratch,
-        compiler_params=pltpu.CompilerParams(collective_id=0, has_side_effects=True, vmem_limit_bytes=67043328),
-        name="adafactor_step",
-    )(*acts, *w_in, *r_in, *c_in, hyper)
+        scratch_shapes=[pltpu.SemaphoreType.DMA((4,)), pltpu.SemaphoreType.DMA((n_row,)), pltpu.SemaphoreType.DMA((4,))],
+        compiler_params=pltpu.CompilerParams(vmem_limit_bytes=WRITE_LIMIT),
+        name="write_out",
+    )(*held)
     new_w = [o.reshape(w.shape) for o, w in zip(outs[:4], w_list)]
-    new_r = [o.reshape(r.shape) for o, r in zip(outs[4:8], r_list)]
-    new_c = [o.reshape(c.shape) for o, c in zip(outs[8:], c_list)]
-    return tuple(part for trio in zip(new_w, new_r, new_c) for part in trio)
+    return tuple(part for trio in zip(new_w, outs[4:8], outs[8:]) for part in trio)
 
 
 def solution(mesh):

time: 106 us -> 88.9 us (0.84)
  local copies, waits for them, and re-layouts: 14.8 us -> 0 us
  other arithmetic: 3.88 us -> 0 us
  Pallas kernels: 86.7 us -> 88.2 us
    unnamed x19 -> x0, local copies, waits for them, and re-layouts: 10.9 us -> none
    pallas_call x3 -> x0, other arithmetic: 3.88 us -> none  [fused_step(): pl.pallas_call(functools.partial(kernel, mats, dp_size, col_size, row_siz...]
    reshape x3 -> x0, local copies, waits for them, and re-layouts: 3.86 us -> none  [the longest x2 2.59 us: fused_step(): c_in = [c.reshape(1, mat.n) for c, mat in zip(c_list, mats)]]
    pallas_call x0 -> x1, Pallas kernels: none -> 2.34 us  [fused_step(): pl.pallas_call(functools.partial(write_kernel, mats), out_shape=w_shape +...]
where the time goes in v2:
time: 88.9 us; the launch traced here: 88.8 us
  Pallas kernels  88.2 us (99%)
    pallas_call x1, Pallas kernels, fused_step(): pl.pallas_call(functools.partial(kernel, mats, dp_size, col_size, row_siz...  85.8 us
    pallas_call x1, Pallas kernels, fused_step(): pl.pallas_call(functools.partial(write_kernel, mats), out_shape=w_shape +...  2.34 us

profile of v2, /device:TPU:1, one launch (start us, length us, event | category | flops | bytes accessed | tf_op | source)
XLA Modules:
  0.0 88.8 jit_solution(7810747620304987236)
XLA Ops:
  0.7 85.8 %adafactor_step.1 = (f32[8,32,512]{2,1,0:T(8,128)S(1)}, f32[8,32,1280]{2,1,0:T(8,128)S(1)}, f32[8,32,1280]{2,1,0:T(8,128)S(1)}, f32[8,80,512]{2,1,0:T(8,128)S(1)...) custom-call(bf16[4096,256]{1,0:T(8,128)(2,1)} %x_attn.1, bf16[4096,512]{1,0:T(8,128)(2,1)} %dy_attn.1, ...), custom_call_target="tpu_custom_call" | custom-call | tf_op jit(solution)/shard_map/adafactor_step/pallas_call | solution.py:394
  86.5 2.3 %write_out.1 = (f32[8,32,512]{2,1,0:T(8,128)}, f32[8,32,1280]{2,1,0:T(8,128)}, f32[8,32,1280]{2,1,0:T(8,128)}, f32[8,80,512]{2,1,0:T(8,128)}, f32[256]{0:T(256)}...) custom-call(f32[8,32,512]{2,1,0:T(8,128)S(1)} %get-tuple-element.30., ...), custom_call_target="tpu_custom_call" | custom-call | tf_op jit(solution)/shard_map/write_out/pallas_call | solution.py:403

commit v3 on v0

v3 whole, which is shorter than its diff:
```python
import functools
import math
import jax
import jax.numpy as jnp
from jax import lax
from jax.experimental import pallas as pl
from jax.experimental.pallas import tpu as pltpu
from jax.sharding import PartitionSpec as P

EPS_ONE = 1e-30
EPS_TWO = 1e-3
LANES = 128
MESH = pl.DeviceIdType.MESH
N_MAT = 4
VMEM_LIMIT = 58 * 1024 * 1024
WRITE_LIMIT = 16 * 1024 * 1024
PIECES = ((0, 4, 4, False), (1, 4, 2, False), (1, 6, 1, False), (2, 6, 1, False), (2, 4, 1, True), (3, 4, 2, False))


class Mat:
    def __init__(self, m, n, row_size, col_size, row_off, col_off):
        self.m, self.n = m, n
        self.mc = m // 8
        self.m_total, self.n_total = m * row_size, n * col_size
        self.rows = m // LANES
        self.row_off, self.col_off = row_off, col_off


class Piece:
    def __init__(self, k, mat, lo, width, chunks, bent):
        self.k, self.mat, self.lo, self.width, self.chunks, self.bent = k, mat, lo, width, chunks, bent
        self.mc = mat.mc
        self.col_off = mat.col_off + lo
        self.tiles = width // LANES


def remote(src, dst, send_sem, recv_sem, axis, index):
    return pltpu.make_async_remote_copy(src_ref=src, dst_ref=dst, send_sem=send_sem, recv_sem=recv_sem,
                                        device_id={axis: index}, device_id_type=MESH)


def wait_bytes(ref, sem):
    pltpu.make_async_copy(ref, ref, sem).wait()


def size_of(ref):
    return math.prod(ref.shape) * jnp.dtype(ref.dtype).itemsize


def total(value):
    return jnp.sum(jnp.sum(value, axis=0, keepdims=True), axis=1, keepdims=True)


def lanes(at):
    return slice(at * LANES, (at + 1) * LANES)


def kernel(mats, pieces, dp_size, col_size, row_size, *refs):
    refs = list(refs)

    def take(count):
        part = refs[:count]
        del refs[:count]
        return part

    n_p = len(pieces)
    acts = take(7)
    w_hbm, r_hbm, c_hbm = take(N_MAT), take(N_MAT), take(N_MAT)
    hyper_hbm, = take(1)
    w_v = take(N_MAT)
    stat_new, = take(1)
    acts_v = take(7)
    x_turn, = take(1)
    gp, rb, gf, acol = take(n_p), take(n_p), take(N_MAT), take(N_MAT)
    hyper, stat_old, b_row, c_own, c_in, r_in, r_own, z_in, c_all, sz, sy, sx = take(12)
    ruler, in_sem, w_sem, st_sem, hyper_sem, rs_send, rs_mid, rs_root, bc_send, bc_fwd, bc_near, bc_last, bc_far, bc_more, ex_send, ex_recv = take(16)
    n_row = sum(mat.m for mat in mats)
    c_len = c_own.shape[2]
    z = lax.axis_index("dp")
    y = lax.axis_index("col")
    x = lax.axis_index("row")
    zp, zm, z2 = lax.rem(z + 1, 4), lax.rem(z + 3, 4), lax.rem(z + 2, 4)
    tokens = acts[0].shape[0]

    def wait_count(size, sem):
        rows = ruler if size <= size_of(ruler) else acts_v[3].at[:, pl.ds(0, 1024)]
        wait_bytes(rows.at[pl.ds(0, size * rows.shape[0] // size_of(rows))], sem)

    x_of = (0, 2, 2, 5)
    dy_of = (1, 3, 4, 6)
    groups = {}

    def load(a, lo, width, t, chunks, sem):
        tc = tokens // chunks
        at = (pl.ds(t * tc, tc), pl.ds(lo, width))
        pltpu.make_async_copy(acts[a].at[at], acts_v[a].at[at], sem).start()
        return tc * width * acts[a].dtype.itemsize

    for p, piece in enumerate(pieces):
        xa, ya = x_of[piece.k], dy_of[piece.k]
        new_x = piece.lo == 0 and x_of.index(xa) == piece.k
        chunks = piece.chunks
        for t in range(chunks):
            sem = in_sem.at[len(groups)]
            size = load(xa, 0, acts[xa].shape[1], t, chunks, sem) if new_x else 0
            groups[p, t] = (size + load(ya, piece.lo, piece.width, t, chunks, sem), sem)
    for k in range(N_MAT):
        pltpu.make_async_copy(w_hbm[k], w_v[k], w_sem).start()
    hyper_copy = pltpu.make_async_copy(hyper_hbm, hyper, hyper_sem)
    hyper_copy.start()
    for k, mat in enumerate(mats):
        pltpu.make_async_copy(r_hbm[k], stat_old.at[0, pl.ds(mat.row_off * LANES, mat.m)], st_sem).start()
        pltpu.make_async_copy(c_hbm[k], stat_old.at[0, pl.ds(n_row + mat.col_off, mat.n)], st_sem).start()

    barrier = pltpu.get_barrier_semaphore()
    partners = 0
    for axis, me, size in (("dp", z, dp_size), ("col", y, col_size), ("row", x, row_size)):
        for d in range(1, size):
            pl.semaphore_signal(barrier, inc=1, device_id={axis: lax.rem(me + d, size)}, device_id_type=MESH)
            partners += 1

    def matmul_chunk(p, t):
        piece = pieces[p]
        wait_count(*groups[p, t])
        tc = tokens // piece.chunks
        at = pl.ds(t * tc, tc)
        xa = x_of[piece.k]
        if piece.k in (0, 1) and piece.lo == 0:
            x_turn[:, at] = acts_v[xa][at, :].T
        if piece.k == 3:
            left, contract = acts_v[xa][at, :], 0
        else:
            left, contract = x_turn[:, at], 1
        part = lax.dot_general(left, acts_v[dy_of[piece.k]][at, pl.ds(piece.lo, piece.width)],
                               (((contract,), (0,)), ((), ())), preferred_element_type=jnp.float32)
        part = part.reshape(8, piece.mc, piece.width)
        if t == 0:
            gp[p][...] = part
        else:
            gp[p][...] += part

    def own_lines(root):
        return [mat.row_off + root // 2 for mat in mats[:-1]] + [mats[-1].row_off + root + i for i in range(2)]

    def cls(root, mirror):
        return 2 * root + mirror

    def rs_copy(p, i, src, axis_index, recv_sem):
        remote(src, rb[p].at[i], rs_send, recv_sem, "dp", axis_index).start()

    def rs_first(p):
        bent = pieces[p].bent
        inner = (z == 1) | (z == 2)
        to_a, slot_a = (jnp.where(inner, zp, zm), jnp.where(inner, 6, 0)) if bent else (zm, 0)
        to_b, slot_b = (jnp.where(inner, zp, zm), jnp.where(inner, 1, 7)) if bent else (zp, 1)
        rs_copy(p, slot_a, gp[p].at[cls(z2, 0)], to_a, rs_mid.at[p])
        rs_copy(p, slot_b, gp[p].at[cls(z2, 1)], to_b, rs_mid.at[p])

        def direct():
            rs_copy(p, 2, gp[p].at[cls(zp, 0)], zp, rs_root.at[pieces[p].k])
            rs_copy(p, 3, gp[p].at[cls(zm, 1)], zm, rs_root.at[pieces[p].k])

        if not bent:
            direct()
            return

        @pl.when(z < 2)
        def _():
            direct()
            rs_copy(p, 4, gp[p].at[cls(zm, 0)], zm, rs_root.at[pieces[p].k])
            rs_copy(p, 5, gp[p].at[cls(zp, 1)], zp, rs_root.at[pieces[p].k])

    def rs_forward(p):
        def forward(mid, chunk, slot, to):
            rb[p][mid] += gp[p][chunk]
            rs_copy(p, slot, rb[p].at[mid], to, rs_root.at[pieces[p].k])

        def both(count_mid):
            wait_bytes(rb[p].at[pl.ds(0, count_mid)], rs_mid.at[p])
            forward(0, cls(zm, 0), 4, zm)
            forward(1, cls(zp, 1), 5, zp)

        if not pieces[p].bent:
            both(2)
            return

        @pl.when(z >= 2)
        def _():
            both(4)
            forward(6, cls(zp, 0), 2, zp)
            forward(7, cls(zm, 1), 3, zm)

    def rs_finish(p):
        piece = pieces[p]
        mat = piece.mat
        if piece.lo == 0:
            wait_count(size_of(gf[piece.k]) // 2, rs_root.at[piece.k])
        cols = jnp.zeros((1, piece.width), jnp.float32)
        row_iota = lax.broadcasted_iota(jnp.int32, (mat.mc, LANES), 0)
        lane_iota = lax.broadcasted_iota(jnp.int32, (mat.mc, LANES), 1)
        lines = [jnp.zeros((1, LANES), jnp.float32) for _ in range(mat.rows)]
        for mirror in range(2):
            own = cls(z, mirror)
            full = gp[p][own] + rb[p][2 + mirror] + rb[p][4 + mirror]
            gf[piece.k][own, :, piece.lo:piece.lo + piece.width] = full
            sq = full * full + EPS_ONE
            cols = cols + jnp.sum(sq, axis=0, keepdims=True)
            row_part = jnp.broadcast_to(jnp.sum(sq, axis=1, keepdims=True), (mat.mc, LANES))
            first = own * mat.mc
            for a in range(mat.rows):
                hit = (row_iota + first) == (lane_iota + a * LANES)
                lines[a] = lines[a] + jnp.sum(jnp.where(hit, row_part, 0.0), axis=0, keepdims=True)
        for j in range(piece.tiles):
            at = piece.col_off + j * LANES
            c_own[at // c_len, :, at % c_len:at % c_len + LANES] = cols[:, lanes(j)]
        for a in range(mat.rows):
            at = lanes(mat.row_off + a)
            if piece.lo == 0:
                r_in[y, :, at] = lines[a]
            else:
                r_in[y, :, at] += lines[a]

    def bc_copy(k, chunk, axis_index, recv_sem):
        remote(gf[k].at[chunk], gf[k].at[chunk], bc_send, recv_sem, "dp", axis_index).start()

    last = N_MAT - 1

    def bc_part(k, chunk, rows, axis_index, send_sem, recv_sem):
        part = gf[k].at[chunk, pl.ds(*rows)]
        remote(part, part, send_sem, recv_sem, "dp", axis_index).start()

    def bc_lead(k):
        bc_copy(k, cls(z, 0), zp, bc_fwd.at[k])
        bc_copy(k, cls(z, 1), zm, bc_fwd.at[k])

    def bc_rest(k):
        near = (bc_fwd.at[0], bc_near, bc_near, bc_last)[k]
        bc_copy(k, cls(z, 1), zp, near)
        bc_copy(k, cls(z, 0), zm, near)

    half = mats[0].mc // 2

    def bc_forward(k, rows=None):
        if rows is None or rows[0] == 0:
            wait_bytes(gf[k].at[pl.ds(0, 4 if k == 0 else 2)], bc_fwd.at[k])
        far = bc_far if k == last else bc_near
        onward = ((cls(zm, 0), zp), (cls(zp, 1), zm))
        if k > 0:
            for chunk, to in onward:
                bc_part(k, chunk, rows or (0, mats[k].mc), to, bc_send, far)
            return
        for chunk, to in onward:
            bc_part(k, chunk, (0, half), to, bc_send, far)

        @pl.when(z != 3)
        def _():
            for chunk, to in onward:
                bc_part(k, chunk, (half, half), to, bc_more, far)

        @pl.when(z == 1)
        def _():
            for chunk, to in ((cls(zm, 1), zp), (cls(zp, 0), zm)):
                bc_part(k, chunk, (half, half), to, bc_more, far)

    slots = {}

    def exchange_start(e, axis, me, size, buf, scatter=None):
        slots[e] = buf.at[pl.ds(0, size - 1)]
        for d in range(1, size):
            peer = lax.rem(me + d, size)
            src = buf.at[me] if scatter is None else scatter.at[peer]
            remote(src, buf.at[me], ex_send, ex_recv.at[max(e - 1, 0)], axis, peer).start()

    def exchange_wait(e):
        if e == 0:
            wait_count(size_of(slots[0]) + size_of(slots[1]), ex_recv.at[0])
        else:
            wait_bytes(slots[e], ex_recv.at[e - 1])

    def sum_slots(buf, size):
        value = buf[0]
        for i in range(1, size):
            value = value + buf[i]
        return value

    def matmul(p):
        for t in range(pieces[p].chunks):
            matmul_chunk(p, t)

    matmul(0)
    pl.semaphore_wait(barrier, partners)
    rs_first(0)
    matmul(1)
    rs_first(1)
    matmul(2)
    rs_first(2)
    rs_forward(0)
    matmul(3)
    rs_first(3)
    matmul(4)
    rs_first(4)
    rs_forward(1)
    rs_forward(2)
    matmul(5)
    rs_first(5)
    c_own[...] = jnp.zeros_like(c_own)
    rs_finish(0)
    wait_count(sum(size_of(w) for w in w_v), w_sem)
    hyper_copy.wait()
    wait_bytes(stat_old, st_sem)
    lane = lax.broadcasted_iota(jnp.int32, (1, LANES), 1)
    scal = jnp.zeros((1, LANES), jnp.float32)
    for k in range(N_MAT):
        for mirror in range(2):
            own_w = w_v[k][cls(z, mirror)]
            scal = jnp.where(lane == 4 + k, scal + total(own_w * own_w), scal)
    rs_forward(3)
    rs_finish(1)
    rs_finish(2)
    rs_forward(4)
    rs_forward(5)
    bc_lead(0)
    bc_rest(0)
    rs_finish(3)
    rs_finish(4)
    bc_lead(1)
    bc_rest(1)
    rs_finish(5)
    c_in[x] = c_own[x]
    exchange_start(0, "row", x, row_size, c_in, c_own)
    exchange_start(1, "col", y, col_size, r_in)
    exchange_wait(0)
    z_in[z, :, 0:c_len] = sum_slots(c_in, row_size)
    r_own[...] = sum_slots(r_in, col_size)
    for i, line in enumerate(own_lines(z)):
        z_in[z, :, c_len + i * LANES:c_len + (i + 1) * LANES] = r_own[:, pl.ds(pl.multiple_of(line * LANES, LANES), LANES)]
    exchange_start(2, "dp", z, dp_size, z_in)
    bc_forward(0)
    bc_lead(2)
    bc_rest(2)
    exchange_wait(2)
    sums = z_in[0, :, 0:c_len]
    for i in range(1, dp_size):
        sums = sums + z_in[i, :, 0:c_len]
    c_all[x] = sums

    def z_line(i, slot):
        return z_in[i, :, c_len + slot * LANES:c_len + (slot + 1) * LANES]

    def row_line(k, a):
        if k < last:
            return z_line(2 * a, k) + z_line(2 * a + 1, k)
        parts = ([z_line(a, last)] if a < dp_size else []) + ([z_line(a - 1, last + 1)] if a > 0 else [])
        return parts[0] + parts[1] if len(parts) == 2 else parts[0]

    exchange_start(3, "row", x, row_size, c_all)
    bc_forward(1, (0, 3 * mats[1].mc // 4))
    beta_two, rho_step, clip_thr = hyper[0], hyper[1], hyper[2]
    row_iota = lax.broadcasted_iota(jnp.int32, (LANES, LANES), 0)
    lane_iota = lax.broadcasted_iota(jnp.int32, (LANES, LANES), 1)
    eye = row_iota == lane_iota
    local_sum = []
    for k, mat in enumerate(mats):
        lines = []
        for a in range(mat.rows):
            at = mat.row_off + a
            mean = row_line(k, a) * (1.0 / mat.n_total)
            lines.append(beta_two * stat_old[:, lanes(at)] + (1.0 - beta_two) * mean)
            stat_new[:, lanes(at)] = lines[-1]
        s_loc = lines[0]
        for line in lines[1:]:
            s_loc = s_loc + line
        s_loc = jnp.sum(s_loc, axis=1, keepdims=True)
        local_sum.append(s_loc)
        for a in range(mat.rows):
            scaled = lax.rsqrt(lines[a] / s_loc)
            column = jnp.sum(jnp.where(eye, jnp.broadcast_to(scaled, (LANES, LANES)), 0.0), axis=1, keepdims=True)
            acol[k][pl.ds(a * LANES, LANES), :] = jnp.broadcast_to(column, (LANES, LANES))
    exchange_wait(3)
    for k, mat in enumerate(mats):
        for j in range(mat.n // LANES):
            at = mat.col_off + j * LANES
            mean = c_all[at // c_len, :, at % c_len:at % c_len + LANES] * (1.0 / mat.m_total)
            new_c = beta_two * stat_old[:, n_row + at:n_row + at + LANES] + (1.0 - beta_two) * mean
            stat_new[:, n_row + at:n_row + at + LANES] = new_c
            b_row[:, at:at + LANES] = lax.rsqrt(new_c)

    def scaled_tile(k, chunk, j):
        mat = mats[k]
        rows = pl.ds(pl.multiple_of(chunk * mat.mc, 8), mat.mc)
        cols = b_row[:, mat.col_off + j * LANES:mat.col_off + (j + 1) * LANES]
        return gf[k][chunk, :, lanes(j)] * acol[k][rows, :] * cols

    for k, mat in enumerate(mats):
        acc = jnp.zeros((mat.mc, LANES), jnp.float32)
        for mirror in range(2):
            for j in range(mat.n // LANES):
                upd = scaled_tile(k, cls(z, mirror), j)
                acc = acc + upd * upd
        scal = jnp.where(lane == k, total(acc), scal)
    sz[z] = scal
    exchange_start(4, "dp", z, dp_size, sz)
    bc_forward(1, (3 * mats[1].mc // 4, mats[1].mc // 4))
    bc_lead(3)
    bc_rest(3)
    bc_forward(2)
    exchange_wait(4)
    sy[y] = sum_slots(sz, dp_size)
    exchange_start(5, "col", y, col_size, sy)
    bc_forward(3)
    exchange_wait(5)
    scal = sum_slots(sy, col_size)
    for k in range(N_MAT):
        scal = jnp.where(lane == 8 + k, jnp.broadcast_to(local_sum[k], (1, LANES)), scal)
    sx[x] = scal
    exchange_start(6, "row", x, row_size, sx)
    exchange_wait(6)
    table = jnp.concatenate([sx[i] for i in range(row_size)], axis=0)
    t_lane = lax.broadcasted_iota(jnp.int32, (row_size, LANES), 1)

    def pick(at):
        return jnp.sum(jnp.where(t_lane == at, table, 0.0), axis=1, keepdims=True)

    factors = []
    for k, mat in enumerate(mats):
        s_each = pick(8 + k)
        s_all = jnp.sum(s_each, axis=0, keepdims=True)
        count = 1.0 / (mat.m_total * mat.n_total)
        u_sq = jnp.sum((s_all / s_each) * pick(k), axis=0, keepdims=True)
        w_sq = jnp.sum(pick(4 + k), axis=0, keepdims=True)
        u_rms = jnp.sqrt(u_sq * count)
        w_rms = jnp.sqrt(w_sq * count)
        step = rho_step * jnp.maximum(EPS_TWO, w_rms) / jnp.maximum(1.0, u_rms / clip_thr)
        factors.append(step * jnp.sqrt(s_all / local_sum[k]))

    moved = sum(size_of(g) for g in gf) * 6 // 8

    def update(k, chunk):
        for j in range(mats[k].n // LANES):
            w_v[k][chunk, :, lanes(j)] = w_v[k][chunk, :, lanes(j)] - factors[k] * scaled_tile(k, chunk, j)

    for k in range(N_MAT):
        for chunk in (cls(z, 0), cls(z, 1), cls(zm, 0), cls(zp, 1)):
            update(k, chunk)
    wait_count(sum(size_of(gf[k].at[pl.ds(0, 2 if k == 0 else 4)]) for k in range(last)), bc_near)
    wait_bytes(gf[last].at[pl.ds(0, 2)], bc_last)
    for k in range(N_MAT):
        update(k, cls(zm, 1))
        update(k, cls(zp, 0))
        if k == last:
            wait_count(moved, rs_send)
            wait_count(sum(size_of(slot) for slot in slots.values()), ex_send)
            wait_bytes(gf[k].at[pl.ds(0, 2)], bc_far)
        update(k, cls(z2, 0))
        update(k, cls(z2, 1))
    chunk_size = size_of(gf[0].at[0])
    wait_count(moved - chunk_size, bc_send)

    @pl.when(z == 1)
    def _():
        wait_count(2 * chunk_size, bc_more)

    @pl.when((z == 0) | (z == 2))
    def _():
        wait_count(chunk_size, bc_more)


def write_kernel(mats, w0, w1, w2, w3, stat_new,
                 o0, o1, o2, o3, ro0, ro1, ro2, ro3, co0, co1, co2, co3, w_sem, r_sem, c_sem):
    n_row = sum(mat.m for mat in mats)
    copies = [pltpu.make_async_copy(src, dst, w_sem.at[k])
              for k, (src, dst) in enumerate(zip((w0, w1, w2, w3), (o0, o1, o2, o3)))]
    for k, mat in enumerate(mats):
        r_out = (ro0, ro1, ro2, ro3)[k]
        c_out = (co0, co1, co2, co3)[k]
        copies.append(pltpu.make_async_copy(stat_new.at[0, pl.ds(mat.row_off * LANES, mat.m)], r_out, r_sem.at[k]))
        copies.append(pltpu.make_async_copy(stat_new.at[0, pl.ds(n_row + mat.col_off, mat.n)], c_out, c_sem.at[k]))
    for copy in copies:
        copy.start()
    for copy in copies:
        copy.wait()


def fused_step(mats, dp_size, col_size, row_size, args):
    (x_attn, dy_attn, x_mlp, dy_gate, dy_up, h_mlp, dy_out, w_list, r_list, c_list, hyper) = args
    any_spec = pl.BlockSpec(memory_space=pl.ANY)
    vmem_spec = pl.BlockSpec(memory_space=pltpu.VMEM)
    f32 = jnp.float32
    pieces = []
    for k, tiles, chunks, bent in PIECES:
        lo = sum(piece.width for piece in pieces if piece.k == k)
        pieces.append(Piece(k, mats[k], lo, tiles * LANES, chunks, bent))
    n_p = len(pieces)
    w_in = [w.reshape(8, mat.mc, mat.n) for w, mat in zip(w_list, mats)]
    acts = (x_attn, dy_attn, x_mlp, dy_gate, dy_up, h_mlp, dy_out)
    n_row = sum(mat.m for mat in mats)
    n_col = sum(mat.n for mat in mats)
    c_len = -(-n_col // (row_size * LANES)) * LANES
    w_shape = [jax.ShapeDtypeStruct(w.shape, f32) for w in w_in]
    held_shape = [pltpu.VMEM(w.shape, f32) for w in w_in] + [pltpu.VMEM((1, n_row + n_col), f32)]
    dma = pltpu.SemaphoreType.DMA
    n_load = sum(piece.chunks for piece in pieces)
    scratch = ([pltpu.VMEM(a.shape, a.dtype) for a in acts]
               + [pltpu.VMEM(x_attn.shape[::-1], x_attn.dtype)]
               + [pltpu.VMEM((8, piece.mc, piece.width), f32) for piece in pieces]
               + [pltpu.VMEM((8 if piece.bent else 6, piece.mc, piece.width), f32) for piece in pieces]
               + [pltpu.VMEM((8, mat.mc, mat.n), f32) for mat in mats]
               + [pltpu.VMEM((mat.m, LANES), f32) for mat in mats]
               + [pltpu.SMEM((3,), f32), pltpu.VMEM((1, n_row + n_col), f32), pltpu.VMEM((1, n_col), f32),
                  pltpu.VMEM((row_size, 1, c_len), f32), pltpu.VMEM((row_size, 1, c_len), f32),
                  pltpu.VMEM((col_size, 1, n_row), f32), pltpu.VMEM((1, n_row), f32),
                  pltpu.VMEM((dp_size, 1, c_len + (N_MAT + 1) * LANES), f32),
                  pltpu.VMEM((row_size, 1, c_len), f32),
                  pltpu.VMEM((dp_size, 1, LANES), f32), pltpu.VMEM((col_size, 1, LANES), f32),
                  pltpu.VMEM((row_size, 1, LANES), f32)]
               + [pltpu.VMEM((256, 1, LANES), f32)]
               + [dma((n_load,)), dma(()), dma(()), dma(()),
                  dma(()), dma((n_p,)), dma((N_MAT,)),
                  dma(()), dma((N_MAT,)), dma(()), dma(()), dma(()), dma(()),
                  dma(()), dma((6,))])
    held = pl.pallas_call(
        functools.partial(kernel, mats, pieces, dp_size, col_size, row_size),
        out_shape=held_shape,
        in_specs=[any_spec] * 20,
        out_specs=[vmem_spec] * 5,
        scratch_shapes=scratch,
        compiler_params=pltpu.CompilerParams(collective_id=0, has_side_effects=True, vmem_limit_bytes=VMEM_LIMIT),
        name="adafactor_step",
    )(*acts, *w_in, *r_list, *c_list, hyper)
    outs = pl.pallas_call(
        functools.partial(write_kernel, mats),
        out_shape=(w_shape + [jax.ShapeDtypeStruct(r.shape, f32) for r in r_list]
                   + [jax.ShapeDtypeStruct(c.shape, f32) for c in c_list]),
        in_specs=[vmem_spec] * 5,
        out_specs=[any_spec] * 12,
        scratch_shapes=[dma((N_MAT,)), dma((N_MAT,)), dma((N_MAT,))],
        compiler_params=pltpu.CompilerParams(vmem_limit_bytes=WRITE_LIMIT),
        name="write_out",
    )(*held)
    new_w = [o.reshape(w.shape) for o, w in zip(outs[:4], w_list)]
    return tuple(part for trio in zip(new_w, outs[4:8], outs[8:]) for part in trio)


def solution(mesh):
    row_size = mesh.shape['row']
    col_size = mesh.shape['col']
    dp_size = mesh.shape['dp']
    act_spec = P('dp', 'row')
    grad_spec = P('dp', 'col')
    w_spec = P('row', 'col')
    row_spec = P('row')
    col_spec = P('col')
    in_specs = (act_spec, grad_spec, act_spec, grad_spec, grad_spec, act_spec, grad_spec,
                w_spec, w_spec, w_spec, w_spec,
                row_spec, col_spec, row_spec, col_spec, row_spec, col_spec, row_spec, col_spec, P())
    out_specs = (w_spec, row_spec, col_spec) * 4

    def per_device(x_attn, dy_attn, x_mlp, dy_gate, dy_up, h_mlp, dy_out, w_attn, w_gate, w_up, w_down,
                   r_attn, c_attn, r_gate, c_gate, r_up, c_up, r_down, c_down, hyper_params):
        w_list = (w_attn, w_gate, w_up, w_down)
        mats = []
        row_off = col_off = 0
        for w in w_list:
            mats.append(Mat(w.shape[0], w.shape[1], row_size, col_size, row_off, col_off))
            row_off += mats[-1].rows
            col_off += mats[-1].n
        return fused_step(mats, dp_size, col_size, row_size,
                          (x_attn, dy_attn, x_mlp, dy_gate, dy_up, h_mlp, dy_out, w_list,
                           (r_attn, r_gate, r_up, r_down), (c_attn, c_gate, c_up, c_down), hyper_params))

    return jax.shard_map(per_device, mesh=mesh, in_specs=in_specs, out_specs=out_specs, check_vma=False)
```

time: 273 us -> 81.9 us (0.30); the launches traced: 268 us -> 81.8 us
  blocking collectives: 94.6 us -> 0 us
  waiting for transfers between devices: 93.5 us -> 0 us
  Pallas kernels: 0 us -> 81.1 us
  other arithmetic: 32.4 us -> 0 us
  between operations: 25.6 us -> 0.66 us
  matrix products: 18.1 us -> 0 us
  local copies, waits for them, and re-layouts: 3.48 us -> 0 us
    psum x3 -> x0, blocking collectives: 94.6 us -> none  [the longest x1 61.9 us: matrix_step(): lax.psum(jnp.sum(update * update), ('row', 'col')) / (m_total * n_total)]
    psum x1 -> x0, waiting for transfers between devices: 93.5 us -> none  [matrix_step(): grad_block = lax.psum(part_grad, 'dp')]
    pallas_call x0 -> x2, Pallas kernels: none -> 81.1 us  [the longest x1 78.9 us: fused_step(): pl.pallas_call(functools.partial(kernel, mats, pieces, dp_size, col_size,...]
    reduce_sum x16 -> x0, other arithmetic: 19.4 us -> none  [the longest x4 7.14 us: matrix_step(): jnp.sum(update * update)]
    dot_general x4 -> x0, matrix products: 18.1 us -> none  [matrix_step(): jnp.einsum('tm,tn->mn', x_block, dy_block, preferred_element_type=jnp.flo...]
    sub x3 -> x0, other arithmetic: 10.3 us -> none  [matrix_step(): return (w_block - step_size * update, new_row, new_col)]
    unnamed x74 -> x0, local copies, waits for them, and re-layouts: 2.82 us -> none
  transfers between devices with their start and end apart: 1 -> 0, of which waited for: 1 -> 0; matrix products, arithmetic and copies ran while one was open for 2% -> 0% of each run, Pallas kernels for 0% -> 0%
where the time goes in v3:
time: 81.9 us; the launch traced here: 81.8 us
  Pallas kernels  81.1 us (99%)
    pallas_call x1, Pallas kernels, fused_step(): pl.pallas_call(functools.partial(kernel, mats, pieces, dp_size, col_size,...  78.9 us
    pallas_call x1, Pallas kernels, fused_step(): pl.pallas_call(functools.partial(write_kernel, mats), out_shape=w_shape +...  2.24 us

profile of v3, /device:TPU:1, one launch (start us, length us, event | category | flops | bytes accessed | tf_op | source)
XLA Modules:
  0.0 81.8 jit_solution(12695904419004546525)
XLA Ops:
  0.7 78.9 %adafactor_step.1 = (f32[8,32,512]{2,1,0:T(8,128)S(1)}, f32[8,32,1280]{2,1,0:T(8,128)S(1)}, f32[8,32,1280]{2,1,0:T(8,128)S(1)}, f32[8,80,512]{2,1,0:T(8,128)S(1)}, f32[1,4992]{1,0:T(1,128)S(1)}) custom-call(bf16[4096,256]{1,0:T(8,128)(2,1)} %refs_0_.1, bf16[4096,512]{1,0:T(8,128)(2,1)} %refs_1_.1, bf16[4096,256]{1,0:T(8,128)(2,1)} %refs_2_.1, ...), custom_call_target="tpu_custom_call" | custom-call | tf_op jit(solution)/shard_map/adafactor_step/pallas_call | solution.py:521
  79.6 2.2 %write_out.1 = (f32[8,32,512]{2,1,0:T(8,128)}, f32[8,32,1280]{2,1,0:T(8,128)}, f32[8,32,1280]{2,1,0:T(8,128)}, f32[8,80,512]{2,1,0:T(8,128)}, f32[256]{0:T(256)}...) custom-call(f32[8,32,512]{2,1,0:T(8,128)S(1)} %get-tuple-element.29., ...), custom_call_target="tpu_custom_call" | custom-call | tf_op jit(solution)/shard_map/write_out/pallas_call | solution.py:530
